TPU v7x, 256 devices: a whole 4x4x8 slice. The times are simulated.
256 devices in a mesh: row: 4 (over y_lo, core), col: 64 (over z, y_hi, x).
Axes of the slice: x: 4, y: 4 (y_hi: 2, y_lo: 2; y = y_hi * 2 + y_lo), z: 8, core: 2. Of those that a mesh axis runs over, the one named last changes fastest.
Arguments:
- image: bfloat16 [8192, 1024], P(('col', 'row')), may hold values from -1 to 1
- text: bfloat16 [8192, 1024], P(('row', 'col')), may hold values from -1 to 1
- audio: bfloat16 [8192, 1024], P(('row', 'col')), may hold values from -1 to 1
Outputs:
- image_grad: float32 [8192, 1024], P(('col', 'row'))
- text_grad: float32 [8192, 1024], P(('row', 'col'))
- audio_grad: float32 [8192, 1024], P(('row', 'col'))
- loss: float32 [], replicated
All inputs are finite; a program needn't handle non-finite values.
Results may differ from a plain program's by a relative error of at most 0.0063.
Values may be sent and summed in bfloat16 or wider, within the bound.
No kernel may reach another device: no remote copies, remote signals or barrier semaphores. Data moves between devices by JAX's collectives and lax.ppermute only.
A program may use at most 64 MiB of HBM per device.

v0:
```python
import functools

import jax
import jax.numpy as jnp
from jax import lax
from jax.sharding import Mesh
from jax.sharding import PartitionSpec as P

ROW = ("row_0", "row_1")
COL = ("col_0", "col_1", "col_2")
ROW_COL = ("row_0", "row_1", "col_0", "col_1", "col_2")
COL_ROW = ("col_0", "col_1", "col_2", "row_0", "row_1")


logit_scale = 20.0
epsilon = 1e-06


def joined_along(parts, dim):
    lengths = list(parts.shape[1:])
    lengths[dim] *= parts.shape[0]
    return jnp.moveaxis(parts, 0, dim).reshape(lengths)


def stacked_from(array, axes, sequence):
    parts = array[None]
    for k in sequence:
        parts = lax.all_gather(parts, axes[k], axis=0, tiled=True)
    carried = [lax.axis_size(axes[k]) for k in reversed(sequence)]
    parts = parts.reshape(*carried, *array.shape)
    turned = sorted(range(len(sequence)), key=lambda place: sequence[len(sequence) - 1 - place])
    return parts.transpose(*turned, *range(len(sequence), parts.ndim)).reshape(-1, *array.shape)


def gather_axes(array, axes, sequence, dim):
    return joined_along(stacked_from(array, axes, sequence), dim)


def side_by_side(arrays, axis, dim, along):
    ends, at = ([], 0)
    for a in arrays[:-1]:
        at += a.shape[along]
        ends.append(at)
    both = jnp.concatenate(arrays, axis=along)
    return tuple(jnp.split(lax.all_gather(both, axis, axis=dim, tiled=True), ends, axis=along))


def copy_for_each(array, axis):
    copies = jnp.broadcast_to(array, (lax.axis_size(axis), *array.shape))
    return lax.all_to_all(copies, axis, split_axis=0, concat_axis=0, tiled=True)


def of_everyone(array, axis):
    return copy_for_each(array, axis).sum(axis=0)


def in_one(arrays, axis):
    ends = [0]
    for a in arrays:
        ends.append(ends[-1] + a.size)
    total = of_everyone(jnp.concatenate([a.ravel() for a in arrays]), axis)
    return tuple((total[b:e].reshape(a.shape) for a, b, e in zip(arrays, ends, ends[1:])))


def split_up(array, dim, peers):
    lengths = array.shape
    parts = array.reshape(*lengths[:dim], peers, lengths[dim] // peers, *lengths[dim + 1 :])
    return jnp.moveaxis(parts, dim, 0)


def summed_on_arrival(array, axis, dim):
    peers = lax.axis_size(axis)
    parts = lax.all_to_all(split_up(array, dim, peers), axis, 0, 0, tiled=True)
    return jnp.sum(parts.astype(jnp.float32), axis=0)


def sum_by_axis(array, axes, dim):
    far, near = axes
    parts = split_up(array, dim, lax.axis_size(far))
    nearer = summed_on_arrival(parts, near, dim + 1)
    arrived = lax.all_to_all(
        nearer.astype(jnp.bfloat16), far, split_axis=0, concat_axis=0, tiled=True
    )
    return arrived.astype(jnp.float32).sum(axis=0)


def over_axes(array, axes):
    return functools.reduce(lax.psum, axes, array)


def normalize(values):
    widened = values.astype(jnp.float32)
    radius = jnp.sqrt(jnp.sum(widened * widened, axis=-1, keepdims=True) + epsilon)
    return (widened / radius, radius)


def through_norm(grad_unit, unit, radius):
    inner = jnp.sum(unit * grad_unit, axis=-1, keepdims=True)
    return (grad_unit - unit * inner) / radius


def scores(left, right):
    return logit_scale * lax.dot_general(
        left, right, (((1,), (1,)), ((), ())), preferred_element_type=jnp.float32
    )


def contract_rows(weights_part, image_tile):
    return lax.dot_general(
        weights_part, image_tile, (((0,), (0,)), ((), ())), preferred_element_type=jnp.float32
    )


def pair_scores(image_tile, text_tile, audio_tile):
    text_scores = scores(image_tile, text_tile)
    audio_scores = scores(image_tile, audio_tile)
    return (
        text_scores,
        audio_scores,
        jnp.exp(text_scores - logit_scale),
        jnp.exp(audio_scores - logit_scale),
    )


def softmax_weights(exp_tile, row_total, column_total, twice_diagonal):
    return (
        exp_tile / row_total[:, None] + exp_tile / column_total[None, :] - twice_diagonal
    ).astype(jnp.bfloat16)


def own_logs(totals, first_row, amount):
    return jnp.sum(jnp.log(lax.dynamic_slice_in_dim(totals, first_row, amount, 0)))


def shards(image, text, audio):
    rows_here = image.shape[0]
    feature_width = image.shape[1]
    image_unit, image_radius = normalize(image)
    text_unit, text_radius = normalize(text)
    audio_unit, audio_radius = normalize(audio)
    image_half = image_unit.astype(jnp.bfloat16)
    text_half = text_unit.astype(jnp.bfloat16)
    audio_half = audio_unit.astype(jnp.bfloat16)
    row_place = lax.axis_index(ROW)
    col_place = lax.axis_index(COL)
    row_count = lax.axis_size(ROW)
    col_count = lax.axis_size(COL)
    image_tile = gather_axes(image_half, COL, (1, 0, 2), 0)
    text_tile, audio_tile = side_by_side((text_half, audio_half), ROW, 0, 1)
    image_local = jnp.arange(col_count * rows_here, dtype=jnp.int32)
    image_ids = (
        image_local // rows_here * row_count + row_place
    ) * rows_here + image_local % rows_here
    pair_local = jnp.arange(row_count * rows_here, dtype=jnp.int32)
    pair_ids = (
        pair_local // rows_here * col_count + col_place
    ) * rows_here + pair_local % rows_here
    text_scores, audio_scores, text_exp, audio_exp = pair_scores(image_tile, text_tile, audio_tile)
    text_row, audio_row = in_one((jnp.sum(text_exp, axis=1), jnp.sum(audio_exp, axis=1)), COL)
    text_column, audio_column = in_one((jnp.sum(text_exp, axis=0), jnp.sum(audio_exp, axis=0)), ROW)
    diagonal = image_ids[:, None] == pair_ids[None, :]
    twice_diagonal = jnp.where(diagonal, 2.0, 0.0).astype(jnp.float32)
    text_weights = softmax_weights(text_exp, text_row, text_column, twice_diagonal)
    audio_weights = softmax_weights(audio_exp, audio_row, audio_column, twice_diagonal)
    image_part = logit_scale * sum_by_axis(
        (
            jnp.dot(text_weights, text_tile, preferred_element_type=jnp.float32)
            + jnp.dot(audio_weights, audio_tile, preferred_element_type=jnp.float32)
        ).astype(jnp.bfloat16),
        (("col_0", "col_1"), "col_2"),
        0,
    )
    partial_value = jnp.concatenate(
        [contract_rows(text_weights, image_tile), contract_rows(audio_weights, image_tile)], axis=1
    )
    pair_part = logit_scale * summed_on_arrival(partial_value.astype(jnp.bfloat16), ROW, 0)
    image_first = col_place * rows_here
    pair_first = row_place * rows_here
    loss_part = (
        own_logs(text_row, image_first, rows_here)
        + own_logs(audio_row, image_first, rows_here)
        + own_logs(text_column, pair_first, rows_here)
        + own_logs(audio_column, pair_first, rows_here)
        - 2.0 * jnp.sum(jnp.where(diagonal, text_scores + audio_scores, 0.0))
    )
    batch_size = rows_here * row_count * col_count
    loss = over_axes(loss_part, ROW_COL) / (4.0 * batch_size) + logit_scale
    return (
        through_norm(image_part, image_unit, image_radius),
        through_norm(pair_part[:, :feature_width], text_unit, text_radius),
        through_norm(pair_part[:, feature_width:], audio_unit, audio_radius),
        loss,
    )


def solution(mesh):
    split = Mesh(mesh.devices.reshape(2, 2, 8, 2, 4), ("row_0", "row_1", "col_0", "col_1", "col_2"))
    placed = (P(COL_ROW, None), P(ROW_COL, None), P(ROW_COL, None))
    return jax.shard_map(
        shards,
        mesh=split,
        in_specs=placed,
        out_specs=(P(COL_ROW, None), P(ROW_COL, None), P(ROW_COL, None), P()),
        check_vma=False,
    )
```

profile of v0, /device:TPU:24, one launch (start us, length us, event | category | flops | bytes accessed | tf_op | source)
XLA Modules:
  0.0 305.4 jit_solution(18293533622989130421)
XLA Ops:
  9.1 6.5 %all-gather = bf16[64,1024]{1,0:T(8,128)(2,1)} all-gather(bf16[32,1024]{1,0:T(8,128)(2,1)S(1)} %fusion.46), channel_id=2, replica_groups=mesh['row_0'=2,'row_1'=2,'col_0'=8,'col_1'=2,'col_2'=4] {'col_1'}, dimensions={0}, use_global_device_ids=true | all-gather | bytes 196608 | tf_op jit(solution)/shard_map/all_gather | solution.py:28
  15.7 41.2 %all-gather.4.cloned.1.call-done = bf16[16,32,1024]{2,1,0:T(8,128)(2,1)} async-done(((bf16[2,32,1024]{2,1,0:T(8,128)(2,1)}), bf16[16,32,1024]{2,1,0:T(8,128)(2,1)}) %all-gather.4.cloned.1.call-update) | async-done | bytes 1048592 | tf_op jit(solution)/shard_map/all_gather | solution.py:28
  60.0 6.5 %all_gather.15 = bf16[128,2048]{1,0:T(8,128)(2,1)S(1)} all-gather(bf16[32,2048]{1,0:T(8,128)(2,1)S(1)} %pad_maximum_fusion.1), channel_id=1, replica_groups=mesh['row_0'=2,'row_1'=2,'col_0'=8,'col_1'=2,'col_2'=4] {'row_0','row_1'}, dimensions={0}, use_global_device_ids=true | all-gather | bytes 655360 | tf_op jit(solution)/shard_map/all_gather | solution.py:45
  66.5 41.4 %all-gather.6.cloned.1.call-done = bf16[64,32,1024]{2,1,0:T(8,128)(2,1)} async-done(((bf16[16,32,1024]{2,1,0:T(8,128)(2,1)}), bf16[64,32,1024]{2,1,0:T(8,128)(2,1)}) %all-gather.6.cloned.1.call-update) | async-done | bytes 4194320 | tf_op jit(solution)/shard_map/all_gather | solution.py:28
  107.9 2.6 copy.12
  112.1 2.4 fusion
  115.1 4.1 %all-to-all-start.1 = ((f32[4,1,256]{2,1,0:T(1,128)}), f32[4,1,256]{2,1,0:T(1,128)S(1)}, u32[]{:S(2)}, u32[]{:S(2)}) async-start(f32[4,1,256]{2,1,0:T(1,128)} %broadcast_in_dim.37), calls=%async_computation.1 | async-start | bytes 8192 | tf_op jit(solution)/shard_map/all_to_all | solution.py:50
  121.0 2.0 broadcast_in_dim.36
  123.0 12.0 %all-to-all-start = ((f32[64,1,4096]{2,1,0:T(1,128)}), f32[64,1,4096]{2,1,0:T(1,128)S(1)}, u32[]{:S(2)}, u32[]{:S(2)}) async-start(f32[64,1,4096]{2,1,0:T(1,128)} %broadcast_in_dim.36), calls=%async_computation | async-start | bytes 2097152 | tf_op jit(solution)/shard_map/all_to_all | solution.py:50
  135.0 28.0 %all-to-all-done = f32[64,1,4096]{2,1,0:T(1,128)S(1)} async-done(((f32[64,1,4096]{2,1,0:T(1,128)}), f32[64,1,4096]{2,1,0:T(1,128)S(1)}, u32[]{:S(2)}, u32[]{:S(2)}) %all-to-all-start) | async-done | bytes 1048608 | tf_op jit(solution)/shard_map/all_to_all | solution.py:50
  163.9 2.5 fusion.10
  167.9 2.4 copy.23
  170.3 4.8 %all-to-all-start.2 = ((bf16[4,16,32,1024]{3,2,1,0:T(8,128)(2,1)}), bf16[4,16,32,1024]{3,2,1,0:T(8,128)(2,1)}, u32[]{:S(2)}, u32[]{:S(2)}) async-start(bf16[4,16,32,1024]{3,2,1,0:T(8,128)(2,1)} %bitcast.27), calls=%async_computation.2 | async-start | bytes 8388608 | tf_op jit(solution)/shard_map/all_to_all | solution.py:73
  175.8 3.3 %convolution_convert_fusion.1 = bf16[4,32,1024]{2,1,0:T(8,128)(2,1)S(1)} fusion(bf16[4,32,2048]{2,1,0:T(8,128)(2,1)S(1)} %bitcast.31, bf16[2048,1024,1]{1,0,2:T(8,128)(2,1)} %bitcast.25), kind=kOutput, calls=%fused_computation.11 | convolution fusion | flops 537001984 | bytes 4980736 | tf_op jit(solution)/shard_map/dot_general | solution.py:109
  180.7 42.2 %all-to-all-done.2 = bf16[4,16,32,1024]{3,2,1,0:T(8,128)(2,1)} async-done(((bf16[4,16,32,1024]{3,2,1,0:T(8,128)(2,1)}), bf16[4,16,32,1024]{3,2,1,0:T(8,128)(2,1)}, u32[]{:S(2)}, u32[]{:S(2)}) %all-to-all-start.2) | async-done | bytes 4194336 | tf_op jit(solution)/shard_map/all_to_all | solution.py:73
  222.8 5.5 %all-to-all-start.4 = ((bf16[4,32,2048]{2,1,0:T(8,128)(2,1)}), bf16[4,32,2048]{2,1,0:T(8,128)(2,1)S(1)}, u32[]{:S(2)}, u32[]{:S(2)}) async-start(bf16[4,32,2048]{2,1,0:T(8,128)(2,1)} %pad_maximum_fusion), calls=%async_computation.4 | async-start | bytes 1048576 | tf_op jit(solution)/shard_map/all_to_all | solution.py:73
  228.3 4.4 %reduce_sum.192 = bf16[16,32,1024]{2,1,0:T(8,128)(2,1)} reduce(bf16[4,16,32,1024]{3,2,1,0:T(8,128)(2,1)} %all-to-all-done.2, bf16[]{:T(256)} %constant.102.clone.1), dimensions={0}, to_apply=%region_9.10 | reduce | flops 1572864 | bytes 5242882 | tf_op jit(solution)/shard_map/reduce_sum | solution.py:74
  232.7 2.7 all-to-all-done.4
  235.5 7.1 %all-to-all-start.3 = ((bf16[16,32,1024]{2,1,0:T(8,128)(2,1)}), bf16[16,32,1024]{2,1,0:T(8,128)(2,1)S(1)}, u32[]{:S(2)}, u32[]{:S(2)}) async-start(bf16[16,32,1024]{2,1,0:T(8,128)(2,1)} %reduce_sum.192), calls=%async_computation.3 | async-start | bytes 2097152 | tf_op jit(solution)/shard_map/all_to_all | solution.py:81
  248.5 5.5 %psum.35 = f32[]{:T(128)} all-reduce(f32[]{:T(128)S(6)} %sub.53), channel_id=1, replica_groups=mesh['row_0'=2,'row_1'=2,'col_0'=8,'col_1'=2,'col_2'=4] {'row_0'}, use_global_device_ids=true, to_apply=%region_20.21 | all-reduce | flops 1 | bytes 8 | tf_op jit(solution)/shard_map/psum | solution.py:88
  254.0 3.1 %psum.36 = f32[]{:T(128)} all-reduce(f32[]{:T(128)} %psum.35), channel_id=1, replica_groups=mesh['row_0'=2,'row_1'=2,'col_0'=8,'col_1'=2,'col_2'=4] {'row_1'}, use_global_device_ids=true, to_apply=%region_21.22 | all-reduce | flops 1 | bytes 8 | tf_op jit(solution)/shard_map/psum | solution.py:88
  257.0 20.9 %psum.37 = f32[]{:T(128)} all-reduce(f32[]{:T(128)} %psum.36), channel_id=1, replica_groups=mesh['row_0'=2,'row_1'=2,'col_0'=8,'col_1'=2,'col_2'=4] {'col_0'}, use_global_device_ids=true, to_apply=%region_22.23 | all-reduce | flops 1 | bytes 8 | tf_op jit(solution)/shard_map/psum | solution.py:88
  277.9 7.1 %psum.38 = f32[]{:T(128)} all-reduce(f32[]{:T(128)} %psum.37), channel_id=1, replica_groups=mesh['row_0'=2,'row_1'=2,'col_0'=8,'col_1'=2,'col_2'=4] {'col_1'}, use_global_device_ids=true, to_apply=%region_23.24 | all-reduce | flops 1 | bytes 8 | tf_op jit(solution)/shard_map/psum | solution.py:88
  285.0 9.5 %psum.39 = f32[]{:T(128)} all-reduce(f32[]{:T(128)} %psum.38), channel_id=1, replica_groups=mesh['row_0'=2,'row_1'=2,'col_0'=8,'col_1'=2,'col_2'=4] {'col_2'}, use_global_device_ids=true, to_apply=%region_24.25 | all-reduce | flops 1 | bytes 8 | tf_op jit(solution)/shard_map/psum | solution.py:88
  (54 shorter events, 18.5 us)
Async XLA Ops:
  7.2 49.8 %all-gather.4.cloned.1.call-start = ((), (), s32[]{:S(2)}) async-start(), calls=%async_computation.5 | async-start | bytes 1179648 | tf_op jit(solution)/shard_map/all_gather | solution.py:28
  15.7 92.2 %all-gather.6.cloned.1.call-start = ((), (), s32[]{:S(2)}) async-start(), calls=%async_computation.6 | async-start | bytes 5242880 | tf_op jit(solution)/shard_map/all_gather | solution.py:28
  66.5 45.6 %copy-start.2 = (bf16[128,2048]{1,0:T(8,128)(2,1)}, bf16[128,2048]{1,0:T(8,128)(2,1)S(1)}, u32[]{:S(2)}) copy-start(bf16[128,2048]{1,0:T(8,128)(2,1)S(1)} %all_gather.15) | copy-start | bytes 1572868
  110.5 4.0 %copy-start = (bf16[8,2,4,32,1024]{4,3,2,1,0:T(8,128)(2,1)}, bf16[8,2,4,32,1024]{4,3,2,1,0:T(8,128)(2,1)S(1)}, u32[]{:S(2)}) copy-start(bf16[8,2,4,32,1024]{4,3,2,1,0:T(8,128)(2,1)S(1)} %copy.12) | copy-start | bytes 12582916
  115.1 5.8 %all-to-all-start.1 = ((f32[4,1,256]{2,1,0:T(1,128)}), f32[4,1,256]{2,1,0:T(1,128)S(1)}, u32[]{:S(2)}, u32[]{:S(2)}) async-start(f32[4,1,256]{2,1,0:T(1,128)} %broadcast_in_dim.37), calls=%async_computation.1 | async-start | bytes 8192 | tf_op jit(solution)/shard_map/all_to_all | solution.py:50
  123.0 40.0 %all-to-all-start = ((f32[64,1,4096]{2,1,0:T(1,128)}), f32[64,1,4096]{2,1,0:T(1,128)S(1)}, u32[]{:S(2)}, u32[]{:S(2)}) async-start(f32[64,1,4096]{2,1,0:T(1,128)} %broadcast_in_dim.36), calls=%async_computation | async-start | bytes 2097152 | tf_op jit(solution)/shard_map/all_to_all | solution.py:50
  163.9 2.5 copy-start.3
  170.3 52.5 %all-to-all-start.2 = ((bf16[4,16,32,1024]{3,2,1,0:T(8,128)(2,1)}), bf16[4,16,32,1024]{3,2,1,0:T(8,128)(2,1)}, u32[]{:S(2)}, u32[]{:S(2)}) async-start(bf16[4,16,32,1024]{3,2,1,0:T(8,128)(2,1)} %bitcast.27), calls=%async_computation.2 | async-start | bytes 8388608 | tf_op jit(solution)/shard_map/all_to_all | solution.py:73
  175.2 3.9 %copy-start.1 = (bf16[8,2,4,32,1024]{4,3,2,1,0:T(8,128)(2,1)S(1)}, bf16[8,2,4,32,1024]{4,3,2,1,0:T(8,128)(2,1)}, u32[]{:S(2)}) copy-start(bf16[8,2,4,32,1024]{4,3,2,1,0:T(8,128)(2,1)} %copy-done) | copy-start | bytes 12582916
  222.8 12.6 %all-to-all-start.4 = ((bf16[4,32,2048]{2,1,0:T(8,128)(2,1)}), bf16[4,32,2048]{2,1,0:T(8,128)(2,1)S(1)}, u32[]{:S(2)}, u32[]{:S(2)}) async-start(bf16[4,32,2048]{2,1,0:T(8,128)(2,1)} %pad_maximum_fusion), calls=%async_computation.4 | async-start | bytes 1048576 | tf_op jit(solution)/shard_map/all_to_all | solution.py:73
  228.3 67.0 %copy-start.5 = (bf16[32,1024]{1,0:T(8,128)(2,1)S(1)}, bf16[32,1024]{1,0:T(8,128)(2,1)}, u32[]{:S(2)}) copy-start(bf16[32,1024]{1,0:T(8,128)(2,1)} %param.4) | copy-start | bytes 196612
  228.3 67.0 %copy-start.6 = (bf16[32,1024]{1,0:T(8,128)(2,1)S(1)}, bf16[32,1024]{1,0:T(8,128)(2,1)}, u32[]{:S(2)}) copy-start(bf16[32,1024]{1,0:T(8,128)(2,1)} %param.5) | copy-start | bytes 196612
  228.3 68.2 %copy-start.4 = (bf16[32,1024]{1,0:T(8,128)(2,1)S(1)}, bf16[32,1024]{1,0:T(8,128)(2,1)}, u32[]{:S(2)}) copy-start(bf16[32,1024]{1,0:T(8,128)(2,1)} %param.3) | copy-start | bytes 196612
  235.5 60.9 %all-to-all-start.3 = ((bf16[16,32,1024]{2,1,0:T(8,128)(2,1)}), bf16[16,32,1024]{2,1,0:T(8,128)(2,1)S(1)}, u32[]{:S(2)}, u32[]{:S(2)}) async-start(bf16[16,32,1024]{2,1,0:T(8,128)(2,1)} %reduce_sum.192), calls=%async_computation.3 | async-start | bytes 2097152 | tf_op jit(solution)/shard_map/all_to_all | solution.py:81
Sparse Core Ops, SparseCore 0:
  15.8 41.1 all-gather.3
  58.8 49.1 all-gather.5
where the time goes:
time: 306 us; the launch traced here: 305 us
  waiting for transfers between devices  157 us (51%)
  blocking collectives  59.1 us (19%)
  starting transfers between devices  33.5 us (11%)
  between operations  19.3 us (6%)
  other arithmetic  16.6 us (5%)
  matrix products  11.9 us (4%)
  local copies, waits for them, and re-layouts  7.67 us (3%)
    all_gather x2, waiting for transfers between devices, stacked_from(): parts = lax.all_gather(parts, axes[k], axis=0, tiled=True)  82.7 us
    psum x5, blocking collectives, over_axes(): return functools.reduce(lax.psum, axes, array)  46 us
    all_to_all x2, waiting for transfers between devices, summed_on_arrival(): parts = lax.all_to_all(split_up(array, dim, peers), axis, 0, 0, tiled=True)  44.9 us
    all_to_all x2, waiting for transfers between devices, copy_for_each(): return lax.all_to_all(copies, axis, split_axis=0, concat_axis=0, tiled=True)  29.7 us
    all_to_all x2, starting transfers between devices, copy_for_each(): return lax.all_to_all(copies, axis, split_axis=0, concat_axis=0, tiled=True)  16.1 us
    all_to_all x2, starting transfers between devices, summed_on_arrival(): parts = lax.all_to_all(split_up(array, dim, peers), axis, 0, 0, tiled=True)  10.3 us
    all_to_all x1, starting transfers between devices, sum_by_axis(): lax.all_to_all(nearer.astype(jnp.bfloat16), far, split_axis=0, concat_axi...  7.08 us
    all_gather x1, blocking collectives, stacked_from(): parts = lax.all_gather(parts, axes[k], axis=0, tiled=True)  6.54 us
  transfers between devices with their start and end apart: 7, of which 6 were waited for; matrix products, arithmetic and copies ran while one was open for 5% of the time, Pallas kernels for 0%

commit v1 on v0

v1 whole, which is shorter than its diff:
```python
import jax
import jax.numpy as jnp
from jax import lax
from jax.sharding import Mesh
from jax.sharding import PartitionSpec as P

AXES = ("y_lo", "core", "z", "y_hi", "x")
COL_ROW = ("z", "y_hi", "x", "y_lo", "core")

logit_scale = 20.0
epsilon = 1e-06


def place(core, x, y, z):
    return (((y % 4 % 2 * 2 + core % 2) * 8 + z % 8) * 2 + y % 4 // 2) * 4 + x % 4


def send(array, move):
    pairs = [
        (place(core, x, y, z), place(*move(core, x, y, z)))
        for core in range(2)
        for x in range(4)
        for y in range(4)
        for z in range(8)
    ]
    return lax.ppermute(array, AXES, pairs)


def swap(array):
    return send(array, lambda core, x, y, z: (1 - core, x, y, z))


def along_first(array, k):
    return send(
        array, lambda core, x, y, z: (core, x, y + k, z) if core else (core, x + k, y, z)
    )


def along_second(array, k):
    return send(
        array, lambda core, x, y, z: (core, x + k, y, z) if core else (core, x, y + k, z)
    )


def along_z(array, k):
    return send(array, lambda core, x, y, z: (core, x, y, z - k if core else z + k))


def up_z(array, k):
    return send(array, lambda core, x, y, z: (core, x, y, z + k))


def normalize(values):
    widened = values.astype(jnp.float32)
    radius = jnp.sqrt(jnp.sum(widened * widened, axis=-1, keepdims=True) + epsilon)
    return (widened / radius, radius)


def through_norm(grad_unit, unit, radius):
    inner = jnp.sum(unit * grad_unit, axis=-1, keepdims=True)
    return (grad_unit - unit * inner) / radius


def dot(left, right, contract):
    return lax.dot_general(left, right, (contract, ((), ())), preferred_element_type=jnp.float32)


def pieces(value, width):
    high = value.astype(jnp.bfloat16).astype(jnp.float32)
    rest = value - high
    middle = rest.astype(jnp.bfloat16).astype(jnp.float32)
    lane = lax.broadcasted_iota(jnp.int32, (8, width), 1)
    return jnp.where(
        lane == 0, high, jnp.where(lane == 1, middle, jnp.where(lane == 2, rest - middle, 0.0))
    ).astype(jnp.bfloat16)


def whole(row):
    return jnp.sum(row[:1, :3].astype(jnp.float32))


def sum_z(rows, plain):
    both = jnp.concatenate([rows, plain], axis=1)
    n = rows.shape[1]

    def turned(got, k):
        return jnp.concatenate([jnp.roll(got[:, :n], -k, axis=0), got[:, n:]], axis=1)

    below, above = up_z(both, 1), up_z(both, -1)
    lower = both + turned(below, 1)
    three = lower + turned(above, -1)
    far_below, far_above = up_z(three, 3), up_z(lower, -3)
    return three + turned(far_below, 3) + turned(far_above, -3)


def sum_plane(parts):
    got = [along_first(parts, k) for k in (1, 3, 2)]
    parts = parts + sum(jnp.roll(g, k, axis=1) for g, k in zip(got, (1, 3, 2)))
    got = [along_second(parts, k) for k in (1, 3, 2)]
    return parts + sum(jnp.roll(g, k, axis=0) for g, k in zip(got, (1, 3, 2)))


def shards(image, text, audio):
    rows = image.shape[0]
    width = image.shape[1]
    core, z, x = lax.axis_index("core"), lax.axis_index("z"), lax.axis_index("x")
    y_lo, y_hi = lax.axis_index("y_lo"), lax.axis_index("y_hi")
    y = y_hi * 2 + y_lo
    first = core == 0

    def ordered(mine, other):
        return jnp.where(
            first, jnp.concatenate([mine, other]), jnp.concatenate([other, mine])
        )

    def own(pair):
        return jnp.where(first, pair[:rows], pair[rows:])

    def partners(pair):
        return jnp.where(first, pair[rows:], pair[:rows])

    image_unit, image_radius = normalize(image)
    text_unit, text_radius = normalize(text)
    audio_unit, audio_radius = normalize(audio)
    image_half = image_unit.astype(jnp.bfloat16)
    text_half = text_unit.astype(jnp.bfloat16)
    audio_half = audio_unit.astype(jnp.bfloat16)

    got = swap(jnp.concatenate([image_half, jnp.where(first, audio_half, text_half)]))
    image_pair = ordered(image_half, got[:rows])
    other_pair = ordered(jnp.where(first, text_half, audio_half), got[rows:])

    near = {k: along_first(other_pair, k) for k in (1, 3, 2)}
    line = jnp.concatenate([other_pair, near[1], near[2], near[3]])
    ups = {4: along_z(image_half, 4)}
    ups.update({k: along_z(image_pair, k) for k in (3, 2, 1)})
    far = {k: along_second(line, k) for k in (1, 3, 2)}
    here = jnp.concatenate([ups[1], ups[2], ups[3], ups[4]])
    image_tile = jnp.concatenate([image_pair, here, swap(here)])
    other_tile = jnp.concatenate([line, far[1], far[2], far[3]])

    half = jnp.arange(2)
    steps = jnp.array([1, 1, 2, 2, 3, 3, 4])
    toward = jnp.where(first, -1, 1)
    image_z = jnp.concatenate([jnp.zeros(2, jnp.int32), steps * toward, -steps * toward]) + z
    image_core = jnp.concatenate([half, half, half, half, core[None], half, half, half, 1 - core[None]])
    image_block = image_z % 8 * 32 + y_hi * 16 + x * 4 + y_lo * 2 + image_core
    a, b = jnp.arange(32) // 2 % 4, jnp.arange(32) // 8
    other_x = (x - jnp.where(first, a, b)) % 4
    other_y = (y - jnp.where(first, b, a)) % 4
    other_block = (
        other_y % 2 * 128 + jnp.arange(32) % 2 * 64 + z * 8 + other_y // 2 * 4 + other_x
    )
    inside = jnp.arange(rows)
    image_ids = (image_block[:, None] * rows + inside[None, :]).reshape(-1)
    other_ids = (other_block[:, None] * rows + inside[None, :]).reshape(-1)
    diagonal = image_ids[:, None] == other_ids[None, :]

    scores = logit_scale * dot(image_tile, other_tile, ((1,), (1,)))
    exps = jnp.exp(scores - logit_scale)
    row_part, column_part = jnp.sum(exps, axis=1), jnp.sum(exps, axis=0)
    matched = jnp.sum(jnp.where(diagonal, scores, 0.0))

    pair = 2 * rows
    head, mine, others = row_part[:pair], row_part[pair : 9 * rows], row_part[9 * rows :]
    lower, upper = jnp.where(first, mine, others), jnp.where(first, others, mine)

    def split(v):
        return v[:pair], v[pair : 2 * pair], v[2 * pair : 3 * pair], v[3 * pair :]

    d1, d2, d3, d4 = split(lower)
    u1, u2, u3, u4 = split(upper)
    cycle = jnp.concatenate([head, u1, u2, u3, d4, u4, d3, d2, d1]).reshape(8, pair)
    summed = sum_z(cycle, jnp.broadcast_to(matched, (8, pair)))
    matched = summed[0, pair]
    cycle = summed[:, :pair]
    lower = jnp.concatenate([cycle[7], cycle[6], cycle[5], cycle[4, :rows]])
    upper = jnp.concatenate([cycle[1], cycle[2], cycle[3], cycle[4, rows:]])
    row_total = jnp.concatenate(
        [cycle[0], jnp.where(first, lower, upper), jnp.where(first, upper, lower)]
    )
    column_total = sum_plane(column_part.reshape(4, 4, pair)).reshape(-1)

    weights = (
        exps / row_total[:, None]
        + exps / column_total[None, :]
        - jnp.where(diagonal, 2.0, 0.0)
    ).astype(jnp.bfloat16)

    row_logs = jnp.sum(jnp.log(row_total)) - 2.0 * matched
    column_logs = jnp.sum(jnp.log(column_total))

    image_part = dot(weights, other_tile, ((1,), (0,)))
    other_part = dot(weights, image_tile, ((0,), (0,)))

    got = swap(
        jnp.concatenate(
            [
                partners(image_part[:pair]).astype(jnp.bfloat16),
                image_part[9 * rows :].astype(jnp.bfloat16),
                pieces(column_logs, width),
            ]
        )
    )
    column_logs = column_logs + whole(got[8 * rows :])
    chip = jnp.concatenate([own(image_part[:pair]), image_part[pair : 9 * rows]]) + got[
        : 8 * rows
    ].astype(jnp.float32)
    note = pieces(column_logs, width)
    ends = {1: (1, 3), 2: (3, 5), 3: (5, 7), 4: (7, 8)}
    back = {
        k: along_z(
            jnp.concatenate([chip[ends[k][0] * rows : ends[k][1] * rows].astype(jnp.bfloat16), note]), -k
        )
        for k in (4, 3, 2, 1)
    }

    note = pieces(row_logs, width)
    bundle = 4 * pair
    got = {
        k: along_second(
            jnp.concatenate([other_part[k * bundle : (k + 1) * bundle].astype(jnp.bfloat16), note]), -k
        )
        for k in (1, 3, 2)
    }
    row_logs = row_logs + sum(whole(got[k][bundle:]) for k in (1, 2, 3))
    line = other_part[:bundle] + sum(got[k][:bundle].astype(jnp.float32) for k in (1, 2, 3))
    note = pieces(row_logs, width)
    got = {
        k: along_first(
            jnp.concatenate([line[k * pair : (k + 1) * pair].astype(jnp.bfloat16), note]), -k
        )
        for k in (1, 3, 2)
    }
    row_logs = row_logs + sum(whole(got[k][pair:]) for k in (1, 2, 3))
    other_sum = line[:pair] + sum(got[k][:pair].astype(jnp.float32) for k in (1, 2, 3))

    near = sum(back[k][:pair].astype(jnp.float32) for k in (1, 2, 3))
    image_sum = chip[:rows] + own(near) + back[4][:rows].astype(jnp.float32)
    logs = row_logs + sum(whole(back[k][pair:]) for k in (1, 2, 3))
    logs = logs + jnp.where(first, column_logs + whole(back[4][rows:]), 0.0)
    got = swap(
        jnp.concatenate(
            [
                partners(near).astype(jnp.bfloat16),
                partners(other_sum).astype(jnp.bfloat16),
                pieces(logs, width),
            ]
        )
    )
    image_sum = image_sum + got[:rows].astype(jnp.float32)
    mine, other = own(other_sum), got[rows:pair].astype(jnp.float32)
    text_sum, audio_sum = jnp.where(first, mine, other), jnp.where(first, other, mine)
    batch_size = rows * 256
    loss = (logs + whole(got[pair:])) / (4.0 * batch_size) + logit_scale
    return (
        through_norm(logit_scale * image_sum, image_unit, image_radius),
        through_norm(logit_scale * text_sum, text_unit, text_radius),
        through_norm(logit_scale * audio_sum, audio_unit, audio_radius),
        loss,
    )


def solution(mesh):
    split = Mesh(mesh.devices.reshape(2, 2, 8, 2, 4), AXES)
    image_spec, other_spec = P(COL_ROW, None), P(AXES, None)
    return jax.shard_map(
        shards,
        mesh=split,
        in_specs=(image_spec, other_spec, other_spec),
        out_specs=(image_spec, other_spec, other_spec, P()),
        check_vma=False,
    )
```

time: 306 us -> 151 us (0.49)
  waiting for transfers between devices: 157 us -> 37.4 us
  blocking collectives: 59.1 us -> 0 us
  starting transfers between devices: 33.5 us -> 54 us
  other arithmetic: 16.6 us -> 28.3 us
  between operations: 19.3 us -> 13.7 us
  matrix products: 11.9 us -> 6.83 us
    all_gather x2 -> x0, waiting for transfers between devices: 82.7 us -> none  [stacked_from(): parts = lax.all_gather(parts, axes[k], axis=0, tiled=True)]
    all_to_all x5 -> x0, waiting for transfers between devices: 74.7 us -> none  [the longest x2 44.9 us: summed_on_arrival(): parts = lax.all_to_all(split_up(array, dim, peers), axis, 0, 0, tiled=True)]
    ppermute x0 -> x34, starting transfers between devices: none -> 54 us  [send(): return lax.ppermute(array, AXES, pairs)]
    psum x5 -> x0, blocking collectives: 46 us -> none  [over_axes(): return functools.reduce(lax.psum, axes, array)]
    ppermute x0 -> x34, waiting for transfers between devices: none -> 37.4 us  [send(): return lax.ppermute(array, AXES, pairs)]
    all_to_all x5 -> x0, starting transfers between devices: 33.5 us -> none  [the longest x2 16.1 us: copy_for_each(): return lax.all_to_all(copies, axis, split_axis=0, concat_axis=0, tiled=True)]
    all_gather x2 -> x0, blocking collectives: 13.1 us -> none  [the longest x1 6.54 us: stacked_from(): parts = lax.all_gather(parts, axes[k], axis=0, tiled=True)]
    dot_general x6 -> x3, matrix products: 11.9 us -> 6.83 us  [dot(): lax.dot_general(left, right, (contract, ((), ())), preferred_element_type...]
  transfers between devices with their start and end apart: 7 -> 34, of which waited for: 6 -> 12; matrix products, arithmetic and copies ran while one was open for 5% -> 10% of each run, Pallas kernels for 0% -> 0%
where the time goes in v1:
time: 151 us; the launch traced here: 148 us
  starting transfers between devices  54 us (36%)
  waiting for transfers between devices  37.4 us (25%)
  other arithmetic  28.3 us (19%)
  between operations  13.7 us (9%)
  local copies, waits for them, and re-layouts  8.24 us (5%)
  matrix products  6.83 us (5%)
    ppermute x34, starting transfers between devices, send(): return lax.ppermute(array, AXES, pairs)  54 us
    ppermute x34, waiting for transfers between devices, send(): return lax.ppermute(array, AXES, pairs)  37.4 us
    reduce_sum x12, other arithmetic, whole(): return jnp.sum(row[:1, :3].astype(jnp.float32))  9.24 us
    dot_general x3, matrix products, dot(): lax.dot_general(left, right, (contract, ((), ())), preferred_element_type...  6.83 us
    unnamed x45, local copies, waits for them, and re-layouts  4.21 us
  transfers between devices with their start and end apart: 34, of which 12 were waited for; matrix products, arithmetic and copies ran while one was open for 10% of the time, Pallas kernels for 0%

profile of v1, /device:TPU:24, one launch (start us, length us, event | category | flops | bytes accessed | tf_op | source)
XLA Modules:
  0.0 148.5 jit_solution(11544775452439356309)
XLA Ops:
  7.6 2.8 %collective-permute-start.8 = (bf16[64,1024]{1,0:T(8,128)(2,1)S(1)}, bf16[64,1024]{1,0:T(8,128)(2,1)S(1)}, u32[]{:S(2)}, u32[]{:S(2)}) collective-permute-start(bf16[64,1024]{1,0:T(8,128)(2,1)S(1)} %get-tuple-element.25), channel_id=1, source_target_pairs={{0,3},{8,11},{16,19},{24,27},{32,35},{40,43},{48,51},{56,59},{128,... | collective-permute-start | bytes 393224 | tf_op jit(solution)/shard_map/ppermute | solution.py:26
  11.2 4.6 %collective-permute-start.3 = (bf16[64,1024]{1,0:T(8,128)(2,1)}, bf16[64,1024]{1,0:T(8,128)(2,1)S(1)}, u32[]{:S(2)}, u32[]{:S(2)}) collective-permute-start(bf16[64,1024]{1,0:T(8,128)(2,1)} %get-tuple-element.27), channel_id=1, source_target_pairs={{0,24},{8,32},{16,40},{24,48},{32,56},{40,0},{48,8},{56,16},{128,1... | collective-permute-start | bytes 393224 | tf_op jit(solution)/shard_map/ppermute | solution.py:26
  15.8 3.6 %collective-permute-start.2 = (bf16[64,1024]{1,0:T(8,128)(2,1)}, bf16[64,1024]{1,0:T(8,128)(2,1)S(1)}, u32[]{:S(2)}, u32[]{:S(2)}) collective-permute-start(bf16[64,1024]{1,0:T(8,128)(2,1)} %get-tuple-element.27), channel_id=1, source_target_pairs={{0,16},{8,24},{16,32},{24,40},{32,48},{40,56},{48,0},{56,8},{128,1... | collective-permute-start | bytes 393224 | tf_op jit(solution)/shard_map/ppermute | solution.py:26
  22.3 4.6 %collective-permute-done.7 = bf16[64,1024]{1,0:T(8,128)(2,1)S(1)} collective-permute-done((bf16[64,1024]{1,0:T(8,128)(2,1)S(1)}, bf16[64,1024]{1,0:T(8,128)(2,1)S(1)}, u32[]{:S(2)}, u32[]{:S(2)}) %collective-permute-start.7) | collective-permute-done | bytes 131104 | tf_op jit(solution)/shard_map/ppermute | solution.py:26
  29.2 6.0 %collective-permute-done.4 = bf16[32,1024]{1,0:T(8,128)(2,1)S(1)} collective-permute-done((bf16[32,1024]{1,0:T(8,128)(2,1)S(1)}, bf16[32,1024]{1,0:T(8,128)(2,1)S(1)}, u32[]{:S(2)}, u32[]{:S(2)}) %collective-permute-start.4) | collective-permute-done | bytes 65568 | tf_op jit(solution)/shard_map/ppermute | solution.py:26
  36.4 2.2 %collective-permute-start.9 = (bf16[256,1024]{1,0:T(8,128)(2,1)S(1)}, bf16[256,1024]{1,0:T(8,128)(2,1)S(1)}, u32[]{:S(2)}, u32[]{:S(2)}) collective-permute-start(bf16[256,1024]{1,0:T(8,128)(2,1)S(1)} %pad_maximum_fusion.4), channel_id=1, source_target_pairs={{0,128},{8,136},{16,144},{24,152},{32,160},{40,168},{48,176},{56,1... | collective-permute-start | bytes 1572872 | tf_op jit(solution)/shard_map/ppermute | solution.py:26
  38.9 1.7 %collective-permute-done.5 = bf16[224,1024]{1,0:T(8,128)(2,1)S(1)} collective-permute-done((bf16[224,1024]{1,0:T(8,128)(2,1)S(1)}, bf16[224,1024]{1,0:T(8,128)(2,1)S(1)}, u32[]{:S(2)}, u32[]{:S(2)}) %collective-permute-start.5) | collective-permute-done | bytes 458784 | tf_op jit(solution)/shard_map/ppermute | solution.py:26
  40.6 8.5 %collective-permute-done.9 = bf16[256,1024]{1,0:T(8,128)(2,1)S(1)} collective-permute-done((bf16[256,1024]{1,0:T(8,128)(2,1)S(1)}, bf16[256,1024]{1,0:T(8,128)(2,1)S(1)}, u32[]{:S(2)}, u32[]{:S(2)}) %collective-permute-start.9) | collective-permute-done | bytes 524320 | tf_op jit(solution)/shard_map/ppermute | solution.py:26
  49.2 2.3 %fusion = (f32[]{:T(128)}, f32[1024]{0:T(1024)S(1)}, f32[512]{0:T(512)S(1)}, f32[512,1024]{1,0:T(8,128)S(1)}) fusion(s32[1024]{0:T(1024)S(1)} %add.423, s32[512]{0:T(512)S(1)} %add.408, bf16[512,1024]{1,0:T(8,128)(2,1)S(1)} %constant_dynamic-update-slice_fusion, bf16[1024,1024]{1,0:T(8,128)(2,1)S(1)} %constant_dynamic-update-slice_fusion.6), kind=kOutput, calls=%fused_computation.2 | convolution fusion | flops 1077410304 | bytes 5255172 | tf_op jit(solution)/shard_map/dot_general | solution.py:65
  52.6 2.3 %collective-permute-start.13 = (f32[8,128]{1,0:T(8,128)S(1)}, f32[8,128]{1,0:T(8,128)S(1)}, u32[]{:S(2)}, u32[]{:S(2)}) collective-permute-start(f32[8,128]{1,0:T(8,128)S(1)} %concatenate.168), channel_id=1, source_target_pairs={{0,56},{8,0},{16,8},{24,16},{32,24},{40,32},{48,40},{56,48},{128,1... | collective-permute-start | bytes 12296 | tf_op jit(solution)/shard_map/ppermute | solution.py:26
  61.4 3.0 %collective-permute-start.14 = (f32[8,128]{1,0:T(8,128)S(1)}, f32[8,128]{1,0:T(8,128)S(1)}, u32[]{:S(2)}, u32[]{:S(2)}) collective-permute-start(f32[8,128]{1,0:T(8,128)S(1)} %get-tuple-element.20), channel_id=1, source_target_pairs={{0,24},{8,32},{16,40},{24,48},{32,56},{40,0},{48,8},{56,16},{128,1... | collective-permute-start | bytes 12296 | tf_op jit(solution)/shard_map/ppermute | solution.py:26
  64.5 3.9 %collective-permute-start.21 = (f32[4,4,64]{2,1,0:T(4,128)S(1)}, f32[4,4,64]{2,1,0:T(4,128)S(1)}, u32[]{:S(2)}, u32[]{:S(2)}) collective-permute-start(f32[4,4,64]{2,1,0:T(4,128)S(1)} %get-tuple-element.22), channel_id=1, source_target_pairs={{0,4},{8,12},{16,20},{24,28},{32,36},{40,44},{48,52},{56,60},{128,... | collective-permute-start | bytes 12296 | tf_op jit(solution)/shard_map/ppermute | solution.py:26
  68.4 3.2 %collective-permute-start.19 = (f32[4,4,64]{2,1,0:T(4,128)S(1)}, f32[4,4,64]{2,1,0:T(4,128)S(1)}, u32[]{:S(2)}, u32[]{:S(2)}) collective-permute-start(f32[4,4,64]{2,1,0:T(4,128)S(1)} %get-tuple-element.22), channel_id=1, source_target_pairs={{0,128},{8,136},{16,144},{24,152},{32,160},{40,168},{48,176},{56,1... | collective-permute-start | bytes 12296 | tf_op jit(solution)/shard_map/ppermute | solution.py:26
  78.2 3.3 %fusion.67 = (bf16[1024,1024]{1,0:T(8,128)(2,1)S(1)}, f32[1024,1024]{1,0:T(8,128)}) fusion(bf16[512,1024]{1,0:T(8,128)(2,1)S(1)} %fusion.2, bf16[512,1024]{1,0:T(8,128)(2,1)S(1)} %copy-done.4), kind=kOutput, calls=%fused_computation.203 | convolution fusion | flops 1074790400 | bytes 8388608 | tf_op jit(solution)/shard_map/dot_general | solution.py:65
  92.0 3.8 %collective-permute-start.25 = (bf16[72,1024]{1,0:T(8,128)(2,1)}, bf16[72,1024]{1,0:T(8,128)(2,1)S(1)}, u32[]{:S(2)}, u32[]{:S(2)}) collective-permute-start(bf16[72,1024]{1,0:T(8,128)(2,1)} %get-tuple-element.45), channel_id=1, source_target_pairs={{0,40},{8,48},{16,56},{24,0},{32,8},{40,16},{48,24},{56,32},{128,1... | collective-permute-start | bytes 442376 | tf_op jit(solution)/shard_map/ppermute | solution.py:26
  95.8 3.8 %collective-permute-start.24 = (bf16[72,1024]{1,0:T(8,128)(2,1)S(1)}, bf16[72,1024]{1,0:T(8,128)(2,1)S(1)}, u32[]{:S(2)}, u32[]{:S(2)}) collective-permute-start(bf16[72,1024]{1,0:T(8,128)(2,1)S(1)} %get-tuple-element.46), channel_id=1, source_target_pairs={{0,48},{8,56},{16,0},{24,8},{32,16},{40,24},{48,32},{56,40},{128,1... | collective-permute-start | bytes 442376 | tf_op jit(solution)/shard_map/ppermute | solution.py:26
  100.8 3.2 %collective-permute-start.29 = (bf16[264,1024]{1,0:T(8,128)(2,1)S(1)}, bf16[264,1024]{1,0:T(8,128)(2,1)S(1)}, u32[]{:S(2)}, u32[]{:S(2)}) collective-permute-start(bf16[264,1024]{1,0:T(8,128)(2,1)S(1)} %get-tuple-element.51), channel_id=1, source_target_pairs={{0,128},{8,136},{16,144},{24,152},{32,160},{40,168},{48,176},{56,1... | collective-permute-start | bytes 1622024 | tf_op jit(solution)/shard_map/ppermute | solution.py:26
  105.9 1.9 %collective-permute-start.27 = (bf16[264,1024]{1,0:T(8,128)(2,1)}, bf16[264,1024]{1,0:T(8,128)(2,1)S(1)}, u32[]{:S(2)}, u32[]{:S(2)}) collective-permute-start(bf16[264,1024]{1,0:T(8,128)(2,1)} %get-tuple-element.53), channel_id=1, source_target_pairs={{0,132},{8,140},{16,148},{24,156},{32,164},{40,172},{48,180},{56,1... | collective-permute-start | bytes 1622024 | tf_op jit(solution)/shard_map/ppermute | solution.py:26
  110.9 4.3 %collective-permute-done.28 = bf16[264,1024]{1,0:T(8,128)(2,1)S(1)} collective-permute-done((bf16[264,1024]{1,0:T(8,128)(2,1)}, bf16[264,1024]{1,0:T(8,128)(2,1)S(1)}, u32[]{:S(2)}, u32[]{:S(2)}) %collective-permute-start.28) | collective-permute-done | bytes 540704 | tf_op jit(solution)/shard_map/ppermute | solution.py:26
  115.7 5.1 %collective-permute-done.27 = bf16[264,1024]{1,0:T(8,128)(2,1)S(1)} collective-permute-done((bf16[264,1024]{1,0:T(8,128)(2,1)}, bf16[264,1024]{1,0:T(8,128)(2,1)S(1)}, u32[]{:S(2)}, u32[]{:S(2)}) %collective-permute-start.27) | collective-permute-done | bytes 540704 | tf_op jit(solution)/shard_map/ppermute | solution.py:26
  124.0 1.5 %fusion.55 = (bf16[256,1024]{1,0:T(8,128)(2,1)S(1)}, f32[256,1024]{1,0:T(8,128)S(1)}) fusion(bf16[264,1024]{1,0:T(8,128)(2,1)S(1)} %collective-permute-done.29, bf16[264,1024]{1,0:T(8,128)(2,1)S(1)} %collective-permute-done.28, bf16[264,1024]{1,0:T(8,128)(2,1)S(1)} %collective-permute-done.27, f32[1024,1024]{1,0:T(8,128)} %get-tuple-element.78), kind=kLoop, calls=%fused_computation.193 | loop fusion | flops 1835008 | bytes 4194304 | tf_op jit(solution)/shard_map/convert.2
  125.8 2.9 %collective-permute-start.31 = (bf16[72,1024]{1,0:T(8,128)(2,1)S(1)}, bf16[72,1024]{1,0:T(8,128)(2,1)S(1)}, u32[]{:S(2)}, u32[]{:S(2)}) collective-permute-start(bf16[72,1024]{1,0:T(8,128)(2,1)S(1)} %get-tuple-element.49), channel_id=1, source_target_pairs={{0,2},{8,10},{16,18},{24,26},{32,34},{40,42},{48,50},{56,58},{128,... | collective-permute-start | bytes 442376 | tf_op jit(solution)/shard_map/ppermute | solution.py:26
  137.8 2.6 %collective-permute-done.32 = bf16[72,1024]{1,0:T(8,128)(2,1)S(1)} collective-permute-done((bf16[72,1024]{1,0:T(8,128)(2,1)S(1)}, bf16[72,1024]{1,0:T(8,128)(2,1)S(1)}, u32[]{:S(2)}, u32[]{:S(2)}) %collective-permute-start.32) | collective-permute-done | bytes 147488 | tf_op jit(solution)/shard_map/ppermute | solution.py:26
  144.8 1.8 %subtract_divide_fusion = (f32[32,1024]{1,0:T(8,128)}, f32[32,1024]{1,0:T(8,128)}, f32[32]{0:T(128)S(1)}, f32[32,1024]{1,0:T(8,128)S(1)}) fusion(f32[32,1024]{1,0:T(8,128)S(1)} %get-tuple-element.9, f32[32]{0:T(128)S(1)} %get-tuple-element.7, f32[32]{0:T(128)S(1)} %get-tuple-element.82, pred[]{:T(512)S(6)} %eq.72, ...), kind=kLoop, calls=%fused_computation.47 | loop fusion | flops 851936 | bytes 1311489 | tf_op jit(solution)/shard_map/div | solution.py:61
  (204 shorter events, 52.0 us)
Async XLA Ops:
  7.6 13.6 %collective-permute-start.8 = (bf16[64,1024]{1,0:T(8,128)(2,1)S(1)}, bf16[64,1024]{1,0:T(8,128)(2,1)S(1)}, u32[]{:S(2)}, u32[]{:S(2)}) collective-permute-start(bf16[64,1024]{1,0:T(8,128)(2,1)S(1)} %get-tuple-element.25), channel_id=1, source_target_pairs={{0,3},{8,11},{16,19},{24,27},{32,35},{40,43},{48,51},{56,59},{128,... | collective-permute-start | bytes 393224 | tf_op jit(solution)/shard_map/ppermute | solution.py:26
  11.2 25.2 %collective-permute-start.3 = (bf16[64,1024]{1,0:T(8,128)(2,1)}, bf16[64,1024]{1,0:T(8,128)(2,1)S(1)}, u32[]{:S(2)}, u32[]{:S(2)}) collective-permute-start(bf16[64,1024]{1,0:T(8,128)(2,1)} %get-tuple-element.27), channel_id=1, source_target_pairs={{0,24},{8,32},{16,40},{24,48},{32,56},{40,0},{48,8},{56,16},{128,1... | collective-permute-start | bytes 393224 | tf_op jit(solution)/shard_map/ppermute | solution.py:26
  15.8 22.8 %collective-permute-start.2 = (bf16[64,1024]{1,0:T(8,128)(2,1)}, bf16[64,1024]{1,0:T(8,128)(2,1)S(1)}, u32[]{:S(2)}, u32[]{:S(2)}) collective-permute-start(bf16[64,1024]{1,0:T(8,128)(2,1)} %get-tuple-element.27), channel_id=1, source_target_pairs={{0,16},{8,24},{16,32},{24,40},{32,48},{40,56},{48,0},{56,8},{128,1... | collective-permute-start | bytes 393224 | tf_op jit(solution)/shard_map/ppermute | solution.py:26
  19.4 19.2 %collective-permute-start.1 = (bf16[64,1024]{1,0:T(8,128)(2,1)}, bf16[64,1024]{1,0:T(8,128)(2,1)S(1)}, u32[]{:S(2)}, u32[]{:S(2)}) collective-permute-start(bf16[64,1024]{1,0:T(8,128)(2,1)} %get-tuple-element.27), channel_id=1, source_target_pairs={{0,8},{8,16},{16,24},{24,32},{32,40},{40,48},{48,56},{56,0},{128,1... | collective-permute-start | bytes 393224 | tf_op jit(solution)/shard_map/ppermute | solution.py:26
  20.4 6.6 %collective-permute-start.7 = (bf16[64,1024]{1,0:T(8,128)(2,1)S(1)}, bf16[64,1024]{1,0:T(8,128)(2,1)S(1)}, u32[]{:S(2)}, u32[]{:S(2)}) collective-permute-start(bf16[64,1024]{1,0:T(8,128)(2,1)S(1)} %get-tuple-element.25), channel_id=1, source_target_pairs={{0,2},{8,10},{16,18},{24,26},{32,34},{40,42},{48,50},{56,58},{128,... | collective-permute-start | bytes 393224 | tf_op jit(solution)/shard_map/ppermute | solution.py:26
  21.2 7.1 %collective-permute-start.6 = (bf16[64,1024]{1,0:T(8,128)(2,1)S(1)}, bf16[64,1024]{1,0:T(8,128)(2,1)S(1)}, u32[]{:S(2)}, u32[]{:S(2)}) collective-permute-start(bf16[64,1024]{1,0:T(8,128)(2,1)S(1)} %get-tuple-element.25), channel_id=1, source_target_pairs={{0,1},{8,9},{16,17},{24,25},{32,33},{40,41},{48,49},{56,57},{128,1... | collective-permute-start | bytes 393224 | tf_op jit(solution)/shard_map/ppermute | solution.py:26
  27.0 8.2 %collective-permute-start.4 = (bf16[32,1024]{1,0:T(8,128)(2,1)S(1)}, bf16[32,1024]{1,0:T(8,128)(2,1)S(1)}, u32[]{:S(2)}, u32[]{:S(2)}) collective-permute-start(bf16[32,1024]{1,0:T(8,128)(2,1)S(1)} %fusion.53), channel_id=1, source_target_pairs={{0,32},{8,40},{16,48},{24,56},{32,0},{40,8},{48,16},{56,24},{128,1... | collective-permute-start | bytes 196616 | tf_op jit(solution)/shard_map/ppermute | solution.py:26
  28.3 20.8 %collective-permute-start.11 = (bf16[256,1024]{1,0:T(8,128)(2,1)S(1)}, bf16[256,1024]{1,0:T(8,128)(2,1)S(1)}, u32[]{:S(2)}, u32[]{:S(2)}) collective-permute-start(bf16[256,1024]{1,0:T(8,128)(2,1)S(1)} %pad_maximum_fusion.4), channel_id=1, source_target_pairs={{0,132},{8,140},{16,148},{24,156},{32,164},{40,172},{48,180},{56,1... | collective-permute-start | bytes 1572872 | tf_op jit(solution)/shard_map/ppermute | solution.py:26
  35.2 13.9 %collective-permute-start.10 = (bf16[256,1024]{1,0:T(8,128)(2,1)S(1)}, bf16[256,1024]{1,0:T(8,128)(2,1)S(1)}, u32[]{:S(2)}, u32[]{:S(2)}) collective-permute-start(bf16[256,1024]{1,0:T(8,128)(2,1)S(1)} %pad_maximum_fusion.4), channel_id=1, source_target_pairs={{0,4},{8,12},{16,20},{24,28},{32,36},{40,44},{48,52},{56,60},{128,... | collective-permute-start | bytes 1572872 | tf_op jit(solution)/shard_map/ppermute | solution.py:26
  36.4 12.7 %collective-permute-start.9 = (bf16[256,1024]{1,0:T(8,128)(2,1)S(1)}, bf16[256,1024]{1,0:T(8,128)(2,1)S(1)}, u32[]{:S(2)}, u32[]{:S(2)}) collective-permute-start(bf16[256,1024]{1,0:T(8,128)(2,1)S(1)} %pad_maximum_fusion.4), channel_id=1, source_target_pairs={{0,128},{8,136},{16,144},{24,152},{32,160},{40,168},{48,176},{56,1... | collective-permute-start | bytes 1572872 | tf_op jit(solution)/shard_map/ppermute | solution.py:26
  55.0 9.4 %collective-permute-start.18 = (f32[4,4,64]{2,1,0:T(4,128)S(1)}, f32[4,4,64]{2,1,0:T(4,128)S(1)}, u32[]{:S(2)}, u32[]{:S(2)}) collective-permute-start(f32[4,4,64]{2,1,0:T(4,128)S(1)} %reshape.308), channel_id=1, source_target_pairs={{0,2},{8,10},{16,18},{24,26},{32,34},{40,42},{48,50},{56,58},{128,... | collective-permute-start | bytes 12296 | tf_op jit(solution)/shard_map/ppermute | solution.py:26
  56.2 8.2 %collective-permute-start.17 = (f32[4,4,64]{2,1,0:T(4,128)S(1)}, f32[4,4,64]{2,1,0:T(4,128)S(1)}, u32[]{:S(2)}, u32[]{:S(2)}) collective-permute-start(f32[4,4,64]{2,1,0:T(4,128)S(1)} %reshape.308), channel_id=1, source_target_pairs={{0,3},{8,11},{16,19},{24,27},{32,35},{40,43},{48,51},{56,59},{128,... | collective-permute-start | bytes 12296 | tf_op jit(solution)/shard_map/ppermute | solution.py:26
  57.3 7.1 %collective-permute-start.16 = (f32[4,4,64]{2,1,0:T(4,128)S(1)}, f32[4,4,64]{2,1,0:T(4,128)S(1)}, u32[]{:S(2)}, u32[]{:S(2)}) collective-permute-start(f32[4,4,64]{2,1,0:T(4,128)S(1)} %reshape.308), channel_id=1, source_target_pairs={{0,1},{8,9},{16,17},{24,25},{32,33},{40,41},{48,49},{56,57},{128,1... | collective-permute-start | bytes 12296 | tf_op jit(solution)/shard_map/ppermute | solution.py:26
  60.5 11.1 %collective-permute-start.15 = (f32[8,128]{1,0:T(8,128)S(1)}, f32[8,128]{1,0:T(8,128)S(1)}, u32[]{:S(2)}, u32[]{:S(2)}) collective-permute-start(f32[8,128]{1,0:T(8,128)S(1)} %get-tuple-element.21), channel_id=1, source_target_pairs={{0,40},{8,48},{16,56},{24,0},{32,8},{40,16},{48,24},{56,32},{128,1... | collective-permute-start | bytes 12296 | tf_op jit(solution)/shard_map/ppermute | solution.py:26
  61.4 10.4 %collective-permute-start.14 = (f32[8,128]{1,0:T(8,128)S(1)}, f32[8,128]{1,0:T(8,128)S(1)}, u32[]{:S(2)}, u32[]{:S(2)}) collective-permute-start(f32[8,128]{1,0:T(8,128)S(1)} %get-tuple-element.20), channel_id=1, source_target_pairs={{0,24},{8,32},{16,40},{24,48},{32,56},{40,0},{48,8},{56,16},{128,1... | collective-permute-start | bytes 12296 | tf_op jit(solution)/shard_map/ppermute | solution.py:26
  64.5 8.8 %collective-permute-start.21 = (f32[4,4,64]{2,1,0:T(4,128)S(1)}, f32[4,4,64]{2,1,0:T(4,128)S(1)}, u32[]{:S(2)}, u32[]{:S(2)}) collective-permute-start(f32[4,4,64]{2,1,0:T(4,128)S(1)} %get-tuple-element.22), channel_id=1, source_target_pairs={{0,4},{8,12},{16,20},{24,28},{32,36},{40,44},{48,52},{56,60},{128,... | collective-permute-start | bytes 12296 | tf_op jit(solution)/shard_map/ppermute | solution.py:26
  90.3 13.7 %collective-permute-start.26 = (bf16[40,1024]{1,0:T(8,128)(2,1)S(1)}, bf16[40,1024]{1,0:T(8,128)(2,1)S(1)}, u32[]{:S(2)}, u32[]{:S(2)}) collective-permute-start(bf16[40,1024]{1,0:T(8,128)(2,1)S(1)} %pad_maximum_fusion.15), channel_id=1, source_target_pairs={{0,32},{8,40},{16,48},{24,56},{32,0},{40,8},{48,16},{56,24},{128,1... | collective-permute-start | bytes 245768 | tf_op jit(solution)/shard_map/ppermute | solution.py:26
  92.0 13.9 %collective-permute-start.25 = (bf16[72,1024]{1,0:T(8,128)(2,1)}, bf16[72,1024]{1,0:T(8,128)(2,1)S(1)}, u32[]{:S(2)}, u32[]{:S(2)}) collective-permute-start(bf16[72,1024]{1,0:T(8,128)(2,1)} %get-tuple-element.45), channel_id=1, source_target_pairs={{0,40},{8,48},{16,56},{24,0},{32,8},{40,16},{48,24},{56,32},{128,1... | collective-permute-start | bytes 442376 | tf_op jit(solution)/shard_map/ppermute | solution.py:26
  95.8 12.0 %collective-permute-start.24 = (bf16[72,1024]{1,0:T(8,128)(2,1)S(1)}, bf16[72,1024]{1,0:T(8,128)(2,1)S(1)}, u32[]{:S(2)}, u32[]{:S(2)}) collective-permute-start(bf16[72,1024]{1,0:T(8,128)(2,1)S(1)} %get-tuple-element.46), channel_id=1, source_target_pairs={{0,48},{8,56},{16,0},{24,8},{32,16},{40,24},{48,32},{56,40},{128,1... | collective-permute-start | bytes 442376 | tf_op jit(solution)/shard_map/ppermute | solution.py:26
  99.6 8.9 %collective-permute-start.23 = (bf16[72,1024]{1,0:T(8,128)(2,1)S(1)}, bf16[72,1024]{1,0:T(8,128)(2,1)S(1)}, u32[]{:S(2)}, u32[]{:S(2)}) collective-permute-start(bf16[72,1024]{1,0:T(8,128)(2,1)S(1)} %get-tuple-element.47), channel_id=1, source_target_pairs={{0,56},{8,0},{16,8},{24,16},{32,24},{40,32},{48,40},{56,48},{128,1... | collective-permute-start | bytes 442376 | tf_op jit(solution)/shard_map/ppermute | solution.py:26
  100.8 22.0 %collective-permute-start.29 = (bf16[264,1024]{1,0:T(8,128)(2,1)S(1)}, bf16[264,1024]{1,0:T(8,128)(2,1)S(1)}, u32[]{:S(2)}, u32[]{:S(2)}) collective-permute-start(bf16[264,1024]{1,0:T(8,128)(2,1)S(1)} %get-tuple-element.51), channel_id=1, source_target_pairs={{0,128},{8,136},{16,144},{24,152},{32,160},{40,168},{48,176},{56,1... | collective-permute-start | bytes 1622024 | tf_op jit(solution)/shard_map/ppermute | solution.py:26
  104.0 11.2 %collective-permute-start.28 = (bf16[264,1024]{1,0:T(8,128)(2,1)}, bf16[264,1024]{1,0:T(8,128)(2,1)S(1)}, u32[]{:S(2)}, u32[]{:S(2)}) collective-permute-start(bf16[264,1024]{1,0:T(8,128)(2,1)} %get-tuple-element.52), channel_id=1, source_target_pairs={{0,4},{8,12},{16,20},{24,28},{32,36},{40,44},{48,52},{56,60},{128,... | collective-permute-start | bytes 1622024 | tf_op jit(solution)/shard_map/ppermute | solution.py:26
  105.9 15.0 %collective-permute-start.27 = (bf16[264,1024]{1,0:T(8,128)(2,1)}, bf16[264,1024]{1,0:T(8,128)(2,1)S(1)}, u32[]{:S(2)}, u32[]{:S(2)}) collective-permute-start(bf16[264,1024]{1,0:T(8,128)(2,1)} %get-tuple-element.53), channel_id=1, source_target_pairs={{0,132},{8,140},{16,148},{24,156},{32,164},{40,172},{48,180},{56,1... | collective-permute-start | bytes 1622024 | tf_op jit(solution)/shard_map/ppermute | solution.py:26
  125.8 9.5 %collective-permute-start.31 = (bf16[72,1024]{1,0:T(8,128)(2,1)S(1)}, bf16[72,1024]{1,0:T(8,128)(2,1)S(1)}, u32[]{:S(2)}, u32[]{:S(2)}) collective-permute-start(bf16[72,1024]{1,0:T(8,128)(2,1)S(1)} %get-tuple-element.49), channel_id=1, source_target_pairs={{0,2},{8,10},{16,18},{24,26},{32,34},{40,42},{48,50},{56,58},{128,... | collective-permute-start | bytes 442376 | tf_op jit(solution)/shard_map/ppermute | solution.py:26
  (29 other events, 207.4 us)

commit v2 on v0

v2 whole, which is shorter than its diff:
```python
import jax
import jax.numpy as jnp
from jax import lax
from jax.experimental import pallas as pl
from jax.experimental.pallas import tpu as pltpu
from jax.sharding import Mesh
from jax.sharding import PartitionSpec as P

AXES = ("y_lo", "core", "z", "y_hi", "x")
COL_ROW = ("z", "y_hi", "x", "y_lo", "core")

logit_scale = 20.0
epsilon = 1e-06
NOTE = 16
CHUNK = 128


def place(core, x, y, z):
    return (((y % 4 % 2 * 2 + core % 2) * 8 + z % 8) * 2 + y % 4 // 2) * 4 + x % 4


def send(array, move):
    pairs = [
        (place(core, x, y, z), place(*move(core, x, y, z)))
        for core in range(2)
        for x in range(4)
        for y in range(4)
        for z in range(8)
    ]
    return lax.ppermute(array, AXES, pairs)


def swap(array):
    return send(array, lambda core, x, y, z: (1 - core, x, y, z))


def along_first(array, k):
    return send(array, lambda core, x, y, z: (core, x, y + k, z) if core else (core, x + k, y, z))


def along_second(array, k):
    return send(array, lambda core, x, y, z: (core, x + k, y, z) if core else (core, x, y + k, z))


def up(array, k):
    return send(array, lambda core, x, y, z: (core, x, y, z - k if core else z + k))


def call(kernel, count, *shapes, last=False, outside=False):
    def space(shape, dtype):
        return jax.ShapeDtypeStruct(shape, dtype) if last else pltpu.VMEM(shape, dtype)

    made = pl.pallas_call(
        kernel,
        out_shape=tuple(space(s, d) for s, d in shapes),
        in_specs=[pl.BlockSpec(memory_space=pltpu.VMEM)] * count,
        out_specs=tuple(pl.BlockSpec(memory_space=pltpu.VMEM) for _ in shapes),
        compiler_params=pltpu.CompilerParams(vmem_limit_bytes=20 * 1024 * 1024),
    )

    def run(*arrays):
        kept_in = pltpu.HBM if outside else pltpu.VMEM
        return made(*(pltpu.with_memory_space_constraint(a, kept_in) for a in arrays))

    return run


def wide(values):
    return values.astype(jnp.float32)


def slim(values):
    return values.astype(jnp.bfloat16)


def normalize(values):
    widened = wide(values)
    radius = jnp.sqrt(jnp.sum(widened * widened, axis=-1, keepdims=True) + epsilon)
    return (widened / radius, radius)


def dot(left, right, contract):
    return lax.dot_general(left, right, (contract, ((), ())), preferred_element_type=jnp.float32)


def pieces(value, width):
    value = jnp.broadcast_to(value, (NOTE, width))
    high = wide(slim(value))
    rest = value - high
    middle = wide(slim(rest))
    lane = lax.broadcasted_iota(jnp.int32, (NOTE, width), 1)
    split = jnp.where(lane == 0, high, jnp.where(lane == 1, middle, rest - middle))
    return slim(jnp.where(lane < 3, split, 0.0))


def whole(rows):
    return jnp.sum(wide(rows)[:1, :128], axis=1, keepdims=True)


def position():
    core, z, x = lax.axis_index("core"), lax.axis_index("z"), lax.axis_index("x")
    return core, x, lax.axis_index("y_hi") * 2 + lax.axis_index("y_lo"), z


def image_ids(at, first_row, count, rows):
    core, x, y, z = at
    r = first_row + lax.broadcasted_iota(jnp.int32, (count, 1), 0)
    block = r // rows
    at_z = (z + jnp.where(core == 0, block // 2, 8 - block // 2)) % 8
    where = at_z * 32 + y // 2 * 16 + x * 4 + y % 2 * 2 + block % 2
    return where * rows + r % rows


def other_ids(at, count, rows):
    core, x, y, z = at
    r = lax.broadcasted_iota(jnp.int32, (1, count), 1)
    block = r // rows
    a, b = block // 2 % 4, block // 8
    at_x = (x - jnp.where(core == 0, a, b) + 4) % 4
    at_y = (y - jnp.where(core == 0, b, a) + 4) % 4
    where = at_y % 2 * 128 + block % 2 * 64 + z * 8 + at_y // 2 * 4 + at_x
    return where * rows + r % rows


def ordered(core, mine, other):
    return jnp.where(core == 0, mine, other), jnp.where(core == 0, other, mine)


def begin_kernel(rows, image, text, audio, sent, kept, units, radii):
    core = lax.axis_index("core")
    found = [normalize(v[...]) for v in (image, text, audio)]
    for k, (unit, radius) in enumerate(found):
        units[k] = unit
        radii[k] = jnp.broadcast_to(radius, radii.shape[1:])
    image_unit, text_unit, audio_unit = (unit for unit, _ in found)
    sent[:rows] = slim(image_unit)
    kept[:rows] = slim(image_unit)
    sent[rows:] = slim(jnp.where(core == 0, audio_unit, text_unit))
    kept[rows:] = slim(jnp.where(core == 0, text_unit, audio_unit))


def pair_kernel(rows, kept, got, images, others):
    core = lax.axis_index("core")
    images[:rows], images[rows:] = ordered(core, kept[:rows], got[:rows])
    others[:rows], others[rows:] = ordered(core, kept[rows:], got[rows:])


def relay_up_kernel(rows, one, two, out):
    core = lax.axis_index("core")
    out[: 2 * rows] = one[...]
    out[2 * rows :] = jnp.where(core == 0, two[:rows], two[rows:])


def below_kernel(rows, one, two, more, out):
    out[: 2 * rows] = one[...]
    out[2 * rows : 4 * rows] = two[...]
    out[4 * rows :] = more[...]


def folded_rows(e, width):
    folded = sum(e[:, j : j + 128] for j in range(0, width, 128))
    return jnp.sum(folded.T, axis=0, keepdims=True)


def score_kernel(rows, pair, below, above, others, images, exps, row_sums, column_sums):
    at = position()
    count, width = images.shape[0], others.shape[0]
    two = 2 * rows
    images[:two] = pair[...]
    for k in range(3):
        images[(k + 1) * two : (k + 2) * two] = above[k * two : (k + 1) * two]
        images[(7 - k) * two : (8 - k) * two] = below[k * two : (k + 1) * two]
    images[4 * two : 4 * two + rows], images[4 * two + rows : 5 * two] = ordered(
        at[0], below[3 * two :], above[3 * two :]
    )
    columns = other_ids(at, width, rows)
    total = jnp.zeros((1, width), jnp.float32)
    matched = jnp.zeros((1, 1), jnp.float32)
    for m in range(0, count, CHUNK):
        s = logit_scale * dot(images[m : m + CHUNK], others[...], ((1,), (1,)))
        e = jnp.exp(s - logit_scale)
        exps[m : m + CHUNK] = e
        row_sums[:, m : m + CHUNK] = folded_rows(e, width)
        total = total + jnp.sum(e, axis=0, keepdims=True)
        hit = image_ids(at, m, CHUNK, rows) == columns
        found = jnp.sum(jnp.where(hit, s, 0.0), axis=0, keepdims=True)
        matched = matched + jnp.sum(found, axis=1, keepdims=True)
    column_sums[...] = total
    row_sums[:, count:] = jnp.broadcast_to(matched, (1, 128))


def turned(values, lanes):
    n = values.shape[1]
    return pltpu.roll(jnp.broadcast_to(values, (8, n)), (n - lanes) % n, 1)[:1]


def turned_rows(got, steps, rows):
    n = got.shape[1] - 128
    return jnp.concatenate([turned(got[:, :n], steps * 2 * rows % n), got[:, n:]], axis=1)


def row_near_kernel(rows, own, below, above, lower, three):
    both = own[...] + turned_rows(below[...], 1, rows)
    lower[...] = both
    three[...] = both + turned_rows(above[...], -1, rows)


def column_near_kernel(rows, own, got1, got2, got3, out):
    step = own.shape[1] // 4
    for b in range(0, own.shape[1], step):
        total = own[:, b : b + step]
        for k, got in ((1, got1), (2, got2), (3, got3)):
            total = total + turned(got[:, b : b + step], step - 2 * rows * k)
        out[:, b : b + step] = total


def sum_log(values):
    return jnp.sum(jnp.log(values), axis=1, keepdims=True)


def other_kernel(rows, exps, images, three, below, above, line, got1, got2, got3, *outs):
    weights, row_logs, column_logs, out = outs
    at = position()
    count, width = exps.shape
    step = width // 4
    row_all = three[...] + turned_rows(below[...], 3, rows) + turned_rows(above[...], -3, rows)
    row_total, matched = row_all[:, :count], row_all[:, count : count + 1]
    column_total = line[...]
    for k, got in ((1, got1), (2, got2), (3, got3)):
        column_total = column_total + turned(got[...], width - step * k)
    columns = other_ids(at, width, rows)
    by_column = 1.0 / column_total
    for m in range(0, count, CHUNK):
        by_row = 1.0 / row_total[:, m : m + CHUNK]
        by_row = jnp.broadcast_to(by_row, (CHUNK, CHUNK)).T[:, :1]
        hit = image_ids(at, m, CHUNK, rows) == columns
        e = exps[m : m + CHUNK]
        weights[m : m + CHUNK] = slim(e * by_row + e * by_column - jnp.where(hit, 2.0, 0.0))
    logs = sum_log(row_total) - 2.0 * matched
    row_logs[...] = jnp.broadcast_to(logs, row_logs.shape)
    column_logs[...] = jnp.broadcast_to(sum_log(column_total), column_logs.shape)
    other_part(weights, images, 1, logs, out)


def other_part(weights, images, b, logs, out):
    step = weights.shape[1] // 4
    out[:step] = slim(dot(weights[:, b * step : (b + 1) * step], images[...], ((0,), (0,))))
    out[step:] = pieces(logs, images.shape[1])


def rest_kernel(rows, weights, images, row_logs, base, out2, out3):
    step = weights.shape[1] // 4
    for b, out in ((3, out3), (2, out2)):
        other_part(weights, images, b, row_logs[:, :1], out)
    base[...] = dot(weights[:, :step], images[...], ((0,), (0,)))


def image_kernel(rows, weights, others, column_logs, sent, kept):
    core = lax.axis_index("core")
    two = 2 * rows

    def part(p, n=1):
        return dot(weights[p * two : (p + n) * two], others[...], ((1,), (0,)))

    own, upper, lower = part(0), part(1, 4), part(5, 3)
    opposite = upper[3 * two :]
    own_mine, own_other = ordered(core, own[:rows], own[rows:])
    far_mine, far_other = ordered(core, opposite[:rows], opposite[rows:])
    sent[:rows] = slim(own_other)
    sent[rows : 7 * rows] = slim(upper[: 3 * two])
    sent[7 * rows : 8 * rows] = slim(far_other)
    sent[8 * rows :] = pieces(column_logs[:, :1], others.shape[1])
    kept[:rows] = own_mine
    for k in range(3):
        kept[rows + k * two : rows + (k + 1) * two] = lower[(2 - k) * two : (3 - k) * two]
    kept[7 * rows :] = far_mine


def chip_kernel(rows, kept, got, column_logs, near, sent, logs):
    near[...] = kept[: 5 * rows] + wide(got[: 5 * rows])
    sent[: 3 * rows] = slim(kept[5 * rows :] + wide(got[5 * rows : 8 * rows]))
    both = column_logs[:, :1] + whole(got[8 * rows :])
    sent[3 * rows :] = pieces(both, kept.shape[1])
    logs[...] = jnp.broadcast_to(both, logs.shape)


def relay_kernel(rows, near, got, logs, one, two):
    pair = 2 * rows
    core = lax.axis_index("core")
    width = near.shape[1]
    one[:pair] = slim(near[rows : rows + pair] + wide(got[:pair]))
    far = wide(got[pair : pair + rows])
    two[:rows] = slim(near[rows + pair : 2 * pair] + jnp.where(core == 0, far, 0.0))
    two[rows:pair] = slim(near[2 * pair :] + jnp.where(core == 0, 0.0, far))
    theirs = whole(got[pair + rows :])
    one[pair:] = pieces(logs[:, :1] + theirs, width)
    two[pair:] = pieces(logs[:, :1] + jnp.where(core == 0, theirs, 0.0), width)


def line_kernel(rows, base, got1, got2, got3, row_logs, kept, logs, out1, out2, out3):
    pair = 2 * rows
    bundle = base.shape[0]
    both = row_logs[:, :1] + whole(got1[bundle:]) + whole(got2[bundle:]) + whole(got3[bundle:])
    note = pieces(both, base.shape[1])
    for k, out in ((1, out1), (3, out3), (2, out2), (0, kept)):
        at = slice(k * pair, (k + 1) * pair)
        part = base[at] + wide(got1[at]) + wide(got2[at]) + wide(got3[at])
        if k:
            out[:pair] = slim(part)
            out[pair:] = note
        else:
            out[...] = part
    logs[...] = jnp.broadcast_to(both, logs.shape)


def gather_kernel(rows, line, got1, got2, got3, near, one, two, row_logs, column_logs, *outs):
    sent, kept, logs = outs
    pair = 2 * rows
    core = lax.axis_index("core")
    other = line[...] + wide(got1[:pair]) + wide(got2[:pair]) + wide(got3[:pair])
    both = wide(one[:pair]) + wide(two[:pair])
    mine, partners = ordered(core, both[:rows], both[rows:])
    kept[:rows] = near[:rows] + mine
    sent[:rows] = slim(partners)
    mine, partners = ordered(core, other[:rows], other[rows:])
    kept[rows:] = mine
    sent[rows:pair] = slim(partners)
    total = row_logs[:, :1] + whole(got1[pair:]) + whole(got2[pair:]) + whole(got3[pair:])
    total = total + whole(one[pair:]) + whole(two[pair:])
    total = total + jnp.where(core == 0, column_logs[:, :1], 0.0)
    sent[pair:] = pieces(total, line.shape[1])
    logs[...] = jnp.broadcast_to(total, logs.shape)


def end_kernel(rows, kept, got, logs, units, radii, image_out, text_out, audio_out, loss):
    core = lax.axis_index("core")
    sums = (kept[:rows] + wide(got[:rows]), *ordered(core, kept[rows:], wide(got[rows : 2 * rows])))
    for k, (total, out) in enumerate(zip(sums, (image_out, text_out, audio_out))):
        unit, radius = units[k], radii[k][:, :1]
        grad = logit_scale * total
        inner = jnp.sum(unit * grad, axis=-1, keepdims=True)
        out[...] = (grad - unit * inner) / radius
    total = logs[:, :1] + whole(got[2 * rows :])
    loss[...] = total / (4.0 * 256 * rows) + logit_scale


def step(image, text, audio):
    rows, width = image.shape
    pair, bundle = 2 * rows, 8 * rows
    bf16, f32 = jnp.bfloat16, jnp.float32

    def local(kernel, arrays, *shapes, **options):
        def bound(*refs):
            kernel(rows, *refs)

        return call(bound, len(arrays), *shapes, **options)(*arrays)

    two = ((pair, width), bf16)
    sent, kept, units, radii = local(
        begin_kernel,
        (image, text, audio),
        two,
        two,
        ((3, rows, width), f32),
        ((3, rows, 128), f32),
        outside=True,
    )
    got = swap(sent)
    image_pair, other_pair = local(pair_kernel, (kept, got), two, two)

    near = {k: along_first(other_pair, k) for k in (1, 3, 2)}
    ups = {k: up(image_pair, k) for k in (1, 2)}
    line = jnp.concatenate([other_pair, near[1], near[2], near[3]])
    far = {k: along_second(line, k) for k in (1, 3, 2)}
    (more,) = local(relay_up_kernel, (ups[1], ups[2]), ((3 * rows, width), bf16))
    more = up(more, 2)
    (below,) = local(below_kernel, (ups[1], ups[2], more), ((7 * rows, width), bf16))
    above = swap(below)
    others = jnp.concatenate([line, far[1], far[2], far[3]])

    count, across = 8 * pair, others.shape[0]
    row_shape, column_shape = ((1, count + 128), f32), ((1, across), f32)
    images, exps, row_sums, column_sums = local(
        score_kernel,
        (image_pair, below, above, others),
        ((count, width), bf16),
        ((count, across), f32),
        row_shape,
        column_shape,
    )
    rows_below, rows_above = up(row_sums, 1), up(row_sums, -1)
    lower, three = local(row_near_kernel, (row_sums, rows_below, rows_above), row_shape, row_shape)
    rows_below, rows_above = up(three, 3), up(lower, -3)
    got = {k: along_first(column_sums, k) for k in (1, 3, 2)}
    (columns,) = local(column_near_kernel, (column_sums, got[1], got[2], got[3]), column_shape)
    got = {k: along_second(columns, k) for k in (1, 3, 2)}

    packet, log = ((bundle + NOTE, width), bf16), ((1, 128), f32)
    weights, row_logs, column_logs, first = local(
        other_kernel,
        (exps, images, three, rows_below, rows_above, columns, got[1], got[2], got[3]),
        ((count, across), bf16),
        log,
        log,
        packet,
    )
    base, *packets = local(
        rest_kernel, (weights, images, row_logs), ((bundle, width), f32), packet, packet
    )
    packets = [first, *packets]
    seconds = {k: along_second(packets[k - 1], -k) for k in (1, 3, 2)}

    sent, kept = local(image_kernel, (weights, others, column_logs), packet, ((bundle, width), f32))
    got = swap(sent)
    around, sent, column_logs = local(
        chip_kernel,
        (kept, got, column_logs),
        ((5 * rows, width), f32),
        ((3 * rows + NOTE, width), bf16),
        log,
    )
    more = up(sent, -2)
    packet = ((pair + NOTE, width), bf16)
    one, two = local(relay_kernel, (around, more, column_logs), packet, packet)
    one, two = up(one, -1), up(two, -2)

    kept, row_logs, *packets = local(
        line_kernel,
        (base, seconds[1], seconds[2], seconds[3], row_logs),
        ((pair, width), f32),
        log,
        packet,
        packet,
        packet,
    )
    firsts = {k: along_first(packets[k - 1], -k) for k in (1, 3, 2)}

    sent, kept, logs = local(
        gather_kernel,
        (kept, firsts[1], firsts[2], firsts[3], around, one, two, row_logs, column_logs),
        packet,
        ((pair, width), f32),
        log,
    )
    got = swap(sent)
    shape = ((rows, width), f32)
    image_grad, text_grad, audio_grad, loss = local(
        end_kernel, (kept, got, logs, units, radii), shape, shape, shape, ((1, 1), f32), last=True
    )
    return image_grad, text_grad, audio_grad, loss.reshape(())


def solution(mesh):
    split = Mesh(mesh.devices.reshape(2, 2, 8, 2, 4), AXES)
    image_spec, other_spec = P(COL_ROW, None), P(AXES, None)
    return jax.shard_map(
        step,
        mesh=split,
        in_specs=(image_spec, other_spec, other_spec),
        out_specs=(image_spec, other_spec, other_spec, P()),
        check_vma=False,
    )
```

time: 306 us -> 103 us (0.34)
  the two profiles are of different devices: /device:TPU:24 before, /device:TPU:1 now
where the time goes in v2:
time: 103 us
  starting transfers between devices  54.9 us (53%)
  waiting for transfers between devices  36.7 us (36%)
  Pallas kernels  10.5 us (10%)
    ppermute x32, starting transfers between devices, send(): return lax.ppermute(array, AXES, pairs)  54.9 us
    ppermute x32, waiting for transfers between devices, send(): return lax.ppermute(array, AXES, pairs)  36.7 us
    pallas_call x15, Pallas kernels, run(): made(*(pltpu.with_memory_space_constraint(a, kept_in) for a in arrays))  10.5 us
  transfers between devices with their start and end apart: 32, of which 17 were waited for; matrix products, arithmetic and copies ran while one was open for 0% of the time, Pallas kernels for 2%

profile of v2, /device:TPU:1, one launch (start us, length us, event | category | flops | bytes accessed | tf_op | source)
XLA Modules:
  0.0 103.0 jit_solution(12707466363708285633)
XLA Ops:
  1.7 3.3 %collective-permute-start = (bf16[64,1024]{1,0:T(8,128)(2,1)S(1)}, bf16[64,1024]{1,0:T(8,128)(2,1)S(1)}, u32[]{:S(2)}, u32[]{:S(2)}) collective-permute-start(bf16[64,1024]{1,0:T(8,128)(2,1)S(1)} %get-tuple-element.43), channel_id=1, source_target_pairs={{0,64},{8,72},{16,80},{24,88},{32,96},{40,104},{48,112},{56,120},{... | collective-permute-start | bytes 393224 | tf_op jit(solution)/shard_map/ppermute | solution.py:30
  6.1 2.7 %collective-permute-start.7 = (bf16[64,1024]{1,0:T(8,128)(2,1)S(1)}, bf16[64,1024]{1,0:T(8,128)(2,1)S(1)}, u32[]{:S(2)}, u32[]{:S(2)}) collective-permute-start(bf16[64,1024]{1,0:T(8,128)(2,1)S(1)} %get-tuple-element.45), channel_id=1, source_target_pairs={{0,3},{8,11},{16,19},{24,27},{32,35},{40,43},{48,51},{56,59},{128,... | collective-permute-start | bytes 393224 | tf_op jit(solution)/shard_map/ppermute | solution.py:30
  8.8 2.6 %collective-permute-done.5 = bf16[64,1024]{1,0:T(8,128)(2,1)S(1)} collective-permute-done((bf16[64,1024]{1,0:T(8,128)(2,1)S(1)}, bf16[64,1024]{1,0:T(8,128)(2,1)S(1)}, u32[]{:S(2)}, u32[]{:S(2)}) %collective-permute-start.5) | collective-permute-done | bytes 131104 | tf_op jit(solution)/shard_map/ppermute | solution.py:30
  11.4 2.9 %collective-permute-done.6 = bf16[64,1024]{1,0:T(8,128)(2,1)S(1)} collective-permute-done((bf16[64,1024]{1,0:T(8,128)(2,1)S(1)}, bf16[64,1024]{1,0:T(8,128)(2,1)S(1)}, u32[]{:S(2)}, u32[]{:S(2)}) %collective-permute-start.6) | collective-permute-done | bytes 131104 | tf_op jit(solution)/shard_map/ppermute | solution.py:30
  14.5 5.4 %collective-permute-start.2 = (bf16[64,1024]{1,0:T(8,128)(2,1)S(1)}, bf16[64,1024]{1,0:T(8,128)(2,1)S(1)}, u32[]{:S(2)}, u32[]{:S(2)}) collective-permute-start(bf16[64,1024]{1,0:T(8,128)(2,1)S(1)} %get-tuple-element.44.refs_0_), channel_id=1, source_target_pairs={{0,16},{8,24},{16,32},{24,40},{32,48},{40,56},{48,0},{56,8},{128,1... | collective-permute-start | bytes 393224 | tf_op jit(solution)/shard_map/ppermute | solution.py:30
  20.6 2.7 %collective-permute-start.9 = (bf16[256,1024]{1,0:T(8,128)(2,1)S(1)}, bf16[256,1024]{1,0:T(8,128)(2,1)S(1)}, u32[]{:S(2)}, u32[]{:S(2)}) collective-permute-start(bf16[256,1024]{1,0:T(8,128)(2,1)S(1)} %get-tuple-element.80), channel_id=1, source_target_pairs={{0,4},{8,12},{16,20},{24,28},{32,36},{40,44},{48,52},{56,60},{128,... | collective-permute-start | bytes 1572872 | tf_op jit(solution)/shard_map/ppermute | solution.py:30
  24.7 2.6 %collective-permute-start.3 = (bf16[96,1024]{1,0:T(8,128)(2,1)S(1)}, bf16[96,1024]{1,0:T(8,128)(2,1)S(1)}, u32[]{:S(2)}, u32[]{:S(2)}) collective-permute-start(bf16[96,1024]{1,0:T(8,128)(2,1)S(1)} %shard_map.68), channel_id=1, source_target_pairs={{0,16},{8,24},{16,32},{24,40},{32,48},{40,56},{48,0},{56,8},{128,1... | collective-permute-start | bytes 589832 | tf_op jit(solution)/shard_map/ppermute | solution.py:30
  27.3 1.8 %collective-permute-start.10 = (bf16[256,1024]{1,0:T(8,128)(2,1)S(1)}, bf16[256,1024]{1,0:T(8,128)(2,1)S(1)}, u32[]{:S(2)}, u32[]{:S(2)}) collective-permute-start(bf16[256,1024]{1,0:T(8,128)(2,1)S(1)} %get-tuple-element.80), channel_id=1, source_target_pairs={{0,132},{8,140},{16,148},{24,156},{32,164},{40,172},{48,180},{56,1... | collective-permute-start | bytes 1572872 | tf_op jit(solution)/shard_map/ppermute | solution.py:30
  29.1 2.6 %collective-permute-done.3.refs_2_ = bf16[96,1024]{1,0:T(8,128)(2,1)S(1)} collective-permute-done((bf16[96,1024]{1,0:T(8,128)(2,1)S(1)}, bf16[96,1024]{1,0:T(8,128)(2,1)S(1)}, u32[]{:S(2)}, u32[]{:S(2)}) %collective-permute-start.3) | collective-permute-done | bytes 196640 | tf_op jit(solution)/shard_map/ppermute | solution.py:30
  31.7 5.9 %collective-permute-start.4 = (bf16[224,1024]{1,0:T(8,128)(2,1)S(1)}, bf16[224,1024]{1,0:T(8,128)(2,1)S(1)}, u32[]{:S(2)}, u32[]{:S(2)}) collective-permute-start(bf16[224,1024]{1,0:T(8,128)(2,1)S(1)} %shard_map.69.refs_1_), channel_id=1, source_target_pairs={{0,64},{8,72},{16,80},{24,88},{32,96},{40,104},{48,112},{56,120},{... | collective-permute-start | bytes 1376264 | tf_op jit(solution)/shard_map/ppermute | solution.py:30
  39.1 3.4 %shard_map.70 = (bf16[512,1024]{1,0:T(8,128)(2,1)S(1)}, f32[512,1024]{1,0:T(8,128)S(1)}, f32[1,640]{1,0:T(1,128)S(1)}, f32[1,1024]{1,0:T(1,128)S(1)}) custom-call(bf16[64,1024]{1,0:T(8,128)(2,1)S(1)} %get-tuple-element.44.refs_0_, bf16[224,1024]{1,0:T(8,128)(2,1)S(1)} %shard_map.69.refs_1_, bf16[224,1024]{1,0:T(8,128)(2,1)S(1)} %collective-permute-done.4.refs_2_, ...), custom_call_target="tpu_custom_call" | custom-call | tf_op jit(solution)/shard_map/pallas_call | solution.py:63
  43.9 1.7 %collective-permute-start.16 = (f32[1,1024]{1,0:T(1,128)S(1)}, f32[1,1024]{1,0:T(1,128)S(1)}, u32[]{:S(2)}, u32[]{:S(2)}) collective-permute-start(f32[1,1024]{1,0:T(1,128)S(1)} %get-tuple-element.51.refs_0_), channel_id=1, source_target_pairs={{0,2},{8,10},{16,18},{24,26},{32,34},{40,42},{48,50},{56,58},{128,... | collective-permute-start | bytes 12296 | tf_op jit(solution)/shard_map/ppermute | solution.py:30
  46.0 2.7 %collective-permute-start.11 = (f32[1,640]{1,0:T(1,128)S(1)}, f32[1,640]{1,0:T(1,128)S(1)}, u32[]{:S(2)}, u32[]{:S(2)}) collective-permute-start(f32[1,640]{1,0:T(1,128)S(1)} %get-tuple-element.48.refs_0_), channel_id=1, source_target_pairs={{0,8},{8,16},{16,24},{24,32},{32,40},{40,48},{48,56},{56,0},{128,1... | collective-permute-start | bytes 7688 | tf_op jit(solution)/shard_map/ppermute | solution.py:30
  51.9 2.2 %collective-permute-start.14 = (f32[1,640]{1,0:T(1,128)S(1)}, f32[1,640]{1,0:T(1,128)S(1)}, u32[]{:S(2)}, u32[]{:S(2)}) collective-permute-start(f32[1,640]{1,0:T(1,128)S(1)} %get-tuple-element.50), channel_id=1, source_target_pairs={{0,40},{8,48},{16,56},{24,0},{32,8},{40,16},{48,24},{56,32},{128,1... | collective-permute-start | bytes 7688 | tf_op jit(solution)/shard_map/ppermute | solution.py:30
  54.1 2.3 %collective-permute-start.13 = (f32[1,640]{1,0:T(1,128)S(1)}, f32[1,640]{1,0:T(1,128)S(1)}, u32[]{:S(2)}, u32[]{:S(2)}) collective-permute-start(f32[1,640]{1,0:T(1,128)S(1)} %get-tuple-element.49.refs_2_), channel_id=1, source_target_pairs={{0,24},{8,32},{16,40},{24,48},{32,56},{40,0},{48,8},{56,16},{128,1... | collective-permute-start | bytes 7688 | tf_op jit(solution)/shard_map/ppermute | solution.py:30
  61.3 4.9 %collective-permute-start.27 = (bf16[272,1024]{1,0:T(8,128)(2,1)S(1)}, bf16[272,1024]{1,0:T(8,128)(2,1)S(1)}, u32[]{:S(2)}, u32[]{:S(2)}) collective-permute-start(bf16[272,1024]{1,0:T(8,128)(2,1)S(1)} %get-tuple-element.64), channel_id=1, source_target_pairs={{0,64},{8,72},{16,80},{24,88},{32,96},{40,104},{48,112},{56,120},{... | collective-permute-start | bytes 1671176 | tf_op jit(solution)/shard_map/ppermute | solution.py:30
  71.1 3.7 %collective-permute-done.21.refs_1_ = bf16[272,1024]{1,0:T(8,128)(2,1)S(1)} collective-permute-done((bf16[272,1024]{1,0:T(8,128)(2,1)S(1)}, bf16[272,1024]{1,0:T(8,128)(2,1)S(1)}, u32[]{:S(2)}, u32[]{:S(2)}) %collective-permute-start.21) | collective-permute-done | bytes 557088 | tf_op jit(solution)/shard_map/ppermute | solution.py:30
  74.8 3.8 %collective-permute-done.22.refs_2_ = bf16[272,1024]{1,0:T(8,128)(2,1)S(1)} collective-permute-done((bf16[272,1024]{1,0:T(8,128)(2,1)S(1)}, bf16[272,1024]{1,0:T(8,128)(2,1)S(1)}, u32[]{:S(2)}, u32[]{:S(2)}) %collective-permute-start.22) | collective-permute-done | bytes 557088 | tf_op jit(solution)/shard_map/ppermute | solution.py:30
  78.7 5.9 %collective-permute-done.23.refs_3_ = bf16[272,1024]{1,0:T(8,128)(2,1)S(1)} collective-permute-done((bf16[272,1024]{1,0:T(8,128)(2,1)S(1)}, bf16[272,1024]{1,0:T(8,128)(2,1)S(1)}, u32[]{:S(2)}, u32[]{:S(2)}) %collective-permute-start.23) | collective-permute-done | bytes 557088 | tf_op jit(solution)/shard_map/ppermute | solution.py:30
  85.0 2.3 %collective-permute-start.24 = (bf16[80,1024]{1,0:T(8,128)(2,1)S(1)}, bf16[80,1024]{1,0:T(8,128)(2,1)S(1)}, u32[]{:S(2)}, u32[]{:S(2)}) collective-permute-start(bf16[80,1024]{1,0:T(8,128)(2,1)S(1)} %get-tuple-element.59), channel_id=1, source_target_pairs={{0,3},{8,11},{16,19},{24,27},{32,35},{40,43},{48,51},{56,59},{128,... | collective-permute-start | bytes 491528 | tf_op jit(solution)/shard_map/ppermute | solution.py:30
  91.3 1.8 %collective-permute-done.25.refs_2_ = bf16[80,1024]{1,0:T(8,128)(2,1)S(1)} collective-permute-done((bf16[80,1024]{1,0:T(8,128)(2,1)S(1)}, bf16[80,1024]{1,0:T(8,128)(2,1)S(1)}, u32[]{:S(2)}, u32[]{:S(2)}) %collective-permute-start.25) | collective-permute-done | bytes 163872 | tf_op jit(solution)/shard_map/ppermute | solution.py:30
  93.0 2.0 %collective-permute-done.26.refs_3_ = bf16[80,1024]{1,0:T(8,128)(2,1)S(1)} collective-permute-done((bf16[80,1024]{1,0:T(8,128)(2,1)S(1)}, bf16[80,1024]{1,0:T(8,128)(2,1)S(1)}, u32[]{:S(2)}, u32[]{:S(2)}) %collective-permute-start.26) | collective-permute-done | bytes 163872 | tf_op jit(solution)/shard_map/ppermute | solution.py:30
  95.0 2.8 %collective-permute-done.30.refs_6_ = bf16[80,1024]{1,0:T(8,128)(2,1)S(1)} collective-permute-done((bf16[80,1024]{1,0:T(8,128)(2,1)S(1)}, bf16[80,1024]{1,0:T(8,128)(2,1)S(1)}, u32[]{:S(2)}, u32[]{:S(2)}) %collective-permute-start.30) | collective-permute-done | bytes 163872 | tf_op jit(solution)/shard_map/ppermute | solution.py:30
  98.0 3.1 %collective-permute-start.31 = (bf16[80,1024]{1,0:T(8,128)(2,1)S(1)}, bf16[80,1024]{1,0:T(8,128)(2,1)S(1)}, u32[]{:S(2)}, u32[]{:S(2)}) collective-permute-start(bf16[80,1024]{1,0:T(8,128)(2,1)S(1)} %get-tuple-element.72), channel_id=1, source_target_pairs={{0,64},{8,72},{16,80},{24,88},{32,96},{40,104},{48,112},{56,120},{... | collective-permute-start | bytes 491528 | tf_op jit(solution)/shard_map/ppermute | solution.py:30
  (62 shorter events, 27.3 us)
Async XLA Ops:
  6.1 8.3 %collective-permute-start.7 = (bf16[64,1024]{1,0:T(8,128)(2,1)S(1)}, bf16[64,1024]{1,0:T(8,128)(2,1)S(1)}, u32[]{:S(2)}, u32[]{:S(2)}) collective-permute-start(bf16[64,1024]{1,0:T(8,128)(2,1)S(1)} %get-tuple-element.45), channel_id=1, source_target_pairs={{0,3},{8,11},{16,19},{24,27},{32,35},{40,43},{48,51},{56,59},{128,... | collective-permute-start | bytes 393224 | tf_op jit(solution)/shard_map/ppermute | solution.py:30
  8.8 5.6 %collective-permute-start.6 = (bf16[64,1024]{1,0:T(8,128)(2,1)S(1)}, bf16[64,1024]{1,0:T(8,128)(2,1)S(1)}, u32[]{:S(2)}, u32[]{:S(2)}) collective-permute-start(bf16[64,1024]{1,0:T(8,128)(2,1)S(1)} %get-tuple-element.45), channel_id=1, source_target_pairs={{0,2},{8,10},{16,18},{24,26},{32,34},{40,42},{48,50},{56,58},{128,... | collective-permute-start | bytes 393224 | tf_op jit(solution)/shard_map/ppermute | solution.py:30
  14.4 23.2 %collective-permute-start.8 = (bf16[256,1024]{1,0:T(8,128)(2,1)S(1)}, bf16[256,1024]{1,0:T(8,128)(2,1)S(1)}, u32[]{:S(2)}, u32[]{:S(2)}) collective-permute-start(bf16[256,1024]{1,0:T(8,128)(2,1)S(1)} %get-tuple-element.80), channel_id=1, source_target_pairs={{0,128},{8,136},{16,144},{24,152},{32,160},{40,168},{48,176},{56,1... | collective-permute-start | bytes 1572872 | tf_op jit(solution)/shard_map/ppermute | solution.py:30
  14.5 8.8 %collective-permute-start.2 = (bf16[64,1024]{1,0:T(8,128)(2,1)S(1)}, bf16[64,1024]{1,0:T(8,128)(2,1)S(1)}, u32[]{:S(2)}, u32[]{:S(2)}) collective-permute-start(bf16[64,1024]{1,0:T(8,128)(2,1)S(1)} %get-tuple-element.44.refs_0_), channel_id=1, source_target_pairs={{0,16},{8,24},{16,32},{24,40},{32,48},{40,56},{48,0},{56,8},{128,1... | collective-permute-start | bytes 393224 | tf_op jit(solution)/shard_map/ppermute | solution.py:30
  20.6 17.1 %collective-permute-start.9 = (bf16[256,1024]{1,0:T(8,128)(2,1)S(1)}, bf16[256,1024]{1,0:T(8,128)(2,1)S(1)}, u32[]{:S(2)}, u32[]{:S(2)}) collective-permute-start(bf16[256,1024]{1,0:T(8,128)(2,1)S(1)} %get-tuple-element.80), channel_id=1, source_target_pairs={{0,4},{8,12},{16,20},{24,28},{32,36},{40,44},{48,52},{56,60},{128,... | collective-permute-start | bytes 1572872 | tf_op jit(solution)/shard_map/ppermute | solution.py:30
  24.7 6.9 %collective-permute-start.3 = (bf16[96,1024]{1,0:T(8,128)(2,1)S(1)}, bf16[96,1024]{1,0:T(8,128)(2,1)S(1)}, u32[]{:S(2)}, u32[]{:S(2)}) collective-permute-start(bf16[96,1024]{1,0:T(8,128)(2,1)S(1)} %shard_map.68), channel_id=1, source_target_pairs={{0,16},{8,24},{16,32},{24,40},{32,48},{40,56},{48,0},{56,8},{128,1... | collective-permute-start | bytes 589832 | tf_op jit(solution)/shard_map/ppermute | solution.py:30
  27.3 10.4 %collective-permute-start.10 = (bf16[256,1024]{1,0:T(8,128)(2,1)S(1)}, bf16[256,1024]{1,0:T(8,128)(2,1)S(1)}, u32[]{:S(2)}, u32[]{:S(2)}) collective-permute-start(bf16[256,1024]{1,0:T(8,128)(2,1)S(1)} %get-tuple-element.80), channel_id=1, source_target_pairs={{0,132},{8,140},{16,148},{24,156},{32,164},{40,172},{48,180},{56,1... | collective-permute-start | bytes 1572872 | tf_op jit(solution)/shard_map/ppermute | solution.py:30
  31.7 7.4 %collective-permute-start.4 = (bf16[224,1024]{1,0:T(8,128)(2,1)S(1)}, bf16[224,1024]{1,0:T(8,128)(2,1)S(1)}, u32[]{:S(2)}, u32[]{:S(2)}) collective-permute-start(bf16[224,1024]{1,0:T(8,128)(2,1)S(1)} %shard_map.69.refs_1_), channel_id=1, source_target_pairs={{0,64},{8,72},{16,80},{24,88},{32,96},{40,104},{48,112},{56,120},{... | collective-permute-start | bytes 1376264 | tf_op jit(solution)/shard_map/ppermute | solution.py:30
  42.4 6.2 %collective-permute-start.17 = (f32[1,1024]{1,0:T(1,128)S(1)}, f32[1,1024]{1,0:T(1,128)S(1)}, u32[]{:S(2)}, u32[]{:S(2)}) collective-permute-start(f32[1,1024]{1,0:T(1,128)S(1)} %get-tuple-element.51.refs_0_), channel_id=1, source_target_pairs={{0,3},{8,11},{16,19},{24,27},{32,35},{40,43},{48,51},{56,59},{128,... | collective-permute-start | bytes 12296 | tf_op jit(solution)/shard_map/ppermute | solution.py:30
  46.0 5.8 %collective-permute-start.12 = (f32[1,640]{1,0:T(1,128)S(1)}, f32[1,640]{1,0:T(1,128)S(1)}, u32[]{:S(2)}, u32[]{:S(2)}) collective-permute-start(f32[1,640]{1,0:T(1,128)S(1)} %get-tuple-element.48.refs_0_), channel_id=1, source_target_pairs={{0,56},{8,0},{16,8},{24,16},{32,24},{40,32},{48,40},{56,48},{128,1... | collective-permute-start | bytes 7688 | tf_op jit(solution)/shard_map/ppermute | solution.py:30
  46.0 5.8 %collective-permute-start.11 = (f32[1,640]{1,0:T(1,128)S(1)}, f32[1,640]{1,0:T(1,128)S(1)}, u32[]{:S(2)}, u32[]{:S(2)}) collective-permute-start(f32[1,640]{1,0:T(1,128)S(1)} %get-tuple-element.48.refs_0_), channel_id=1, source_target_pairs={{0,8},{8,16},{16,24},{24,32},{32,40},{40,48},{48,56},{56,0},{128,1... | collective-permute-start | bytes 7688 | tf_op jit(solution)/shard_map/ppermute | solution.py:30
  49.4 9.0 %collective-permute-start.20 = (f32[1,1024]{1,0:T(1,128)S(1)}, f32[1,1024]{1,0:T(1,128)S(1)}, u32[]{:S(2)}, u32[]{:S(2)}) collective-permute-start(f32[1,1024]{1,0:T(1,128)S(1)} %shard_map.72.refs_5_), channel_id=1, source_target_pairs={{0,132},{8,140},{16,148},{24,156},{32,164},{40,172},{48,180},{56,1... | collective-permute-start | bytes 12296 | tf_op jit(solution)/shard_map/ppermute | solution.py:30
  50.7 7.6 %collective-permute-start.19 = (f32[1,1024]{1,0:T(1,128)S(1)}, f32[1,1024]{1,0:T(1,128)S(1)}, u32[]{:S(2)}, u32[]{:S(2)}) collective-permute-start(f32[1,1024]{1,0:T(1,128)S(1)} %shard_map.72.refs_5_), channel_id=1, source_target_pairs={{0,4},{8,12},{16,20},{24,28},{32,36},{40,44},{48,52},{56,60},{128,... | collective-permute-start | bytes 12296 | tf_op jit(solution)/shard_map/ppermute | solution.py:30
  51.3 7.0 %collective-permute-start.18 = (f32[1,1024]{1,0:T(1,128)S(1)}, f32[1,1024]{1,0:T(1,128)S(1)}, u32[]{:S(2)}, u32[]{:S(2)}) collective-permute-start(f32[1,1024]{1,0:T(1,128)S(1)} %shard_map.72.refs_5_), channel_id=1, source_target_pairs={{0,128},{8,136},{16,144},{24,152},{32,160},{40,168},{48,176},{56,1... | collective-permute-start | bytes 12296 | tf_op jit(solution)/shard_map/ppermute | solution.py:30
  61.3 8.6 %collective-permute-start.27 = (bf16[272,1024]{1,0:T(8,128)(2,1)S(1)}, bf16[272,1024]{1,0:T(8,128)(2,1)S(1)}, u32[]{:S(2)}, u32[]{:S(2)}) collective-permute-start(bf16[272,1024]{1,0:T(8,128)(2,1)S(1)} %get-tuple-element.64), channel_id=1, source_target_pairs={{0,64},{8,72},{16,80},{24,88},{32,96},{40,104},{48,112},{56,120},{... | collective-permute-start | bytes 1671176 | tf_op jit(solution)/shard_map/ppermute | solution.py:30
  66.2 8.7 %collective-permute-start.21 = (bf16[272,1024]{1,0:T(8,128)(2,1)S(1)}, bf16[272,1024]{1,0:T(8,128)(2,1)S(1)}, u32[]{:S(2)}, u32[]{:S(2)}) collective-permute-start(bf16[272,1024]{1,0:T(8,128)(2,1)S(1)} %get-tuple-element.55), channel_id=1, source_target_pairs={{0,132},{8,140},{16,148},{24,156},{32,164},{40,172},{48,180},{56,1... | collective-permute-start | bytes 1671176 | tf_op jit(solution)/shard_map/ppermute | solution.py:30
  68.4 10.3 %collective-permute-start.22 = (bf16[272,1024]{1,0:T(8,128)(2,1)S(1)}, bf16[272,1024]{1,0:T(8,128)(2,1)S(1)}, u32[]{:S(2)}, u32[]{:S(2)}) collective-permute-start(bf16[272,1024]{1,0:T(8,128)(2,1)S(1)} %get-tuple-element.56), channel_id=1, source_target_pairs={{0,4},{8,12},{16,20},{24,28},{32,36},{40,44},{48,52},{56,60},{128,... | collective-permute-start | bytes 1671176 | tf_op jit(solution)/shard_map/ppermute | solution.py:30
  69.7 14.9 %collective-permute-start.23 = (bf16[272,1024]{1,0:T(8,128)(2,1)S(1)}, bf16[272,1024]{1,0:T(8,128)(2,1)S(1)}, u32[]{:S(2)}, u32[]{:S(2)}) collective-permute-start(bf16[272,1024]{1,0:T(8,128)(2,1)S(1)} %get-tuple-element.57), channel_id=1, source_target_pairs={{0,128},{8,136},{16,144},{24,152},{32,160},{40,168},{48,176},{56,1... | collective-permute-start | bytes 1671176 | tf_op jit(solution)/shard_map/ppermute | solution.py:30
  70.1 18.0 %collective-permute-start.28 = (bf16[112,1024]{1,0:T(8,128)(2,1)S(1)}, bf16[112,1024]{1,0:T(8,128)(2,1)S(1)}, u32[]{:S(2)}, u32[]{:S(2)}) collective-permute-start(bf16[112,1024]{1,0:T(8,128)(2,1)S(1)} %get-tuple-element.66), channel_id=1, source_target_pairs={{0,48},{8,56},{16,0},{24,8},{32,16},{40,24},{48,32},{56,40},{128,1... | collective-permute-start | bytes 688136 | tf_op jit(solution)/shard_map/ppermute | solution.py:30
  85.0 6.3 %collective-permute-start.24 = (bf16[80,1024]{1,0:T(8,128)(2,1)S(1)}, bf16[80,1024]{1,0:T(8,128)(2,1)S(1)}, u32[]{:S(2)}, u32[]{:S(2)}) collective-permute-start(bf16[80,1024]{1,0:T(8,128)(2,1)S(1)} %get-tuple-element.59), channel_id=1, source_target_pairs={{0,3},{8,11},{16,19},{24,27},{32,35},{40,43},{48,51},{56,59},{128,... | collective-permute-start | bytes 491528 | tf_op jit(solution)/shard_map/ppermute | solution.py:30
  87.3 5.8 %collective-permute-start.25 = (bf16[80,1024]{1,0:T(8,128)(2,1)S(1)}, bf16[80,1024]{1,0:T(8,128)(2,1)S(1)}, u32[]{:S(2)}, u32[]{:S(2)}) collective-permute-start(bf16[80,1024]{1,0:T(8,128)(2,1)S(1)} %get-tuple-element.60), channel_id=1, source_target_pairs={{0,2},{8,10},{16,18},{24,26},{32,34},{40,42},{48,50},{56,58},{128,... | collective-permute-start | bytes 491528 | tf_op jit(solution)/shard_map/ppermute | solution.py:30
  88.1 6.9 %collective-permute-start.26 = (bf16[80,1024]{1,0:T(8,128)(2,1)S(1)}, bf16[80,1024]{1,0:T(8,128)(2,1)S(1)}, u32[]{:S(2)}, u32[]{:S(2)}) collective-permute-start(bf16[80,1024]{1,0:T(8,128)(2,1)S(1)} %get-tuple-element.61), channel_id=1, source_target_pairs={{0,1},{8,9},{16,17},{24,25},{32,33},{40,41},{48,49},{56,57},{128,1... | collective-permute-start | bytes 491528 | tf_op jit(solution)/shard_map/ppermute | solution.py:30
  88.3 6.7 %collective-permute-start.29 = (bf16[80,1024]{1,0:T(8,128)(2,1)S(1)}, bf16[80,1024]{1,0:T(8,128)(2,1)S(1)}, u32[]{:S(2)}, u32[]{:S(2)}) collective-permute-start(bf16[80,1024]{1,0:T(8,128)(2,1)S(1)} %get-tuple-element.68), channel_id=1, source_target_pairs={{0,56},{8,0},{16,8},{24,16},{32,24},{40,32},{48,40},{56,48},{128,1... | collective-permute-start | bytes 491528 | tf_op jit(solution)/shard_map/ppermute | solution.py:30
  89.6 8.2 %collective-permute-start.30 = (bf16[80,1024]{1,0:T(8,128)(2,1)S(1)}, bf16[80,1024]{1,0:T(8,128)(2,1)S(1)}, u32[]{:S(2)}, u32[]{:S(2)}) collective-permute-start(bf16[80,1024]{1,0:T(8,128)(2,1)S(1)} %get-tuple-element.69), channel_id=1, source_target_pairs={{0,48},{8,56},{16,0},{24,8},{32,16},{40,24},{48,32},{56,40},{128,1... | collective-permute-start | bytes 491528 | tf_op jit(solution)/shard_map/ppermute | solution.py:30
  (8 other events, 36.8 us)

commit v3 on v2

--- a/solution.py
+++ b/solution.py
@@ -1,3 +1,5 @@
+import math
+
 import jax
 import jax.numpy as jnp
 from jax import lax
@@ -11,7 +13,7 @@
 
 logit_scale = 20.0
 epsilon = 1e-06
-NOTE = 16
+NOTE = 8
 CHUNK = 128
 
 
@@ -111,9 +113,9 @@
     return where * rows + r % rows
 
 
-def other_ids(at, count, rows):
+def other_ids(at, first_row, count, rows):
     core, x, y, z = at
-    r = lax.broadcasted_iota(jnp.int32, (1, count), 1)
+    r = first_row + lax.broadcasted_iota(jnp.int32, (1, count), 1)
     block = r // rows
     a, b = block // 2 % 4, block // 8
     at_x = (x - jnp.where(core == 0, a, b) + 4) % 4
@@ -173,12 +175,13 @@
     images[4 * two : 4 * two + rows], images[4 * two + rows : 5 * two] = ordered(
         at[0], below[3 * two :], above[3 * two :]
     )
-    columns = other_ids(at, width, rows)
+    columns = other_ids(at, 0, width, rows)
     total = jnp.zeros((1, width), jnp.float32)
     matched = jnp.zeros((1, 1), jnp.float32)
+    rate = logit_scale / math.log(2.0)
     for m in range(0, count, CHUNK):
-        s = logit_scale * dot(images[m : m + CHUNK], others[...], ((1,), (1,)))
-        e = jnp.exp(s - logit_scale)
+        s = dot(images[m : m + CHUNK], others[...], ((1,), (1,)))
+        e = jnp.exp2(s * rate - rate)
         exps[m : m + CHUNK] = e
         row_sums[:, m : m + CHUNK] = folded_rows(e, width)
         total = total + jnp.sum(e, axis=0, keepdims=True)
@@ -186,7 +189,7 @@
         found = jnp.sum(jnp.where(hit, s, 0.0), axis=0, keepdims=True)
         matched = matched + jnp.sum(found, axis=1, keepdims=True)
     column_sums[...] = total
-    row_sums[:, count:] = jnp.broadcast_to(matched, (1, 128))
+    row_sums[:, count:] = jnp.broadcast_to(logit_scale * matched, (1, 128))
 
 
 def turned(values, lanes):
@@ -218,9 +221,24 @@
     return jnp.sum(jnp.log(values), axis=1, keepdims=True)
 
 
+def weigh(rows, exps, row_total, column_total, b, out, at_column=0):
+    at = position()
+    count, width = exps.shape
+    step = width // 4
+    here = slice(b * step, (b + 1) * step)
+    there = slice(at_column, at_column + step)
+    columns = other_ids(at, b * step, step, rows)
+    by_column = 1.0 / column_total[:, here]
+    for m in range(0, count, CHUNK):
+        by_row = 1.0 / row_total[:, m : m + CHUNK]
+        by_row = jnp.broadcast_to(by_row, (CHUNK, CHUNK)).T[:, :1]
+        hit = image_ids(at, m, CHUNK, rows) == columns
+        e = exps[m : m + CHUNK, here]
+        out[m : m + CHUNK, there] = slim(e * by_row + e * by_column - jnp.where(hit, 2.0, 0.0))
+
+
 def other_kernel(rows, exps, images, three, below, above, line, got1, got2, got3, *outs):
-    weights, row_logs, column_logs, out = outs
-    at = position()
+    weights, rows_out, columns_out, row_logs, out = outs
     count, width = exps.shape
     step = width // 4
     row_all = three[...] + turned_rows(below[...], 3, rows) + turned_rows(above[...], -3, rows)
@@ -228,52 +246,54 @@
     column_total = line[...]
     for k, got in ((1, got1), (2, got2), (3, got3)):
         column_total = column_total + turned(got[...], width - step * k)
-    columns = other_ids(at, width, rows)
-    by_column = 1.0 / column_total
-    for m in range(0, count, CHUNK):
-        by_row = 1.0 / row_total[:, m : m + CHUNK]
-        by_row = jnp.broadcast_to(by_row, (CHUNK, CHUNK)).T[:, :1]
-        hit = image_ids(at, m, CHUNK, rows) == columns
-        e = exps[m : m + CHUNK]
-        weights[m : m + CHUNK] = slim(e * by_row + e * by_column - jnp.where(hit, 2.0, 0.0))
+    rows_out[...], columns_out[...] = row_total, column_total
+    weigh(rows, exps, row_total, column_total, 1, weights)
     logs = sum_log(row_total) - 2.0 * matched
     row_logs[...] = jnp.broadcast_to(logs, row_logs.shape)
-    column_logs[...] = jnp.broadcast_to(sum_log(column_total), column_logs.shape)
-    other_part(weights, images, 1, logs, out)
-
-
-def other_part(weights, images, b, logs, out):
-    step = weights.shape[1] // 4
-    out[:step] = slim(dot(weights[:, b * step : (b + 1) * step], images[...], ((0,), (0,))))
+    other_part(weights[...], images, logs, out)
+
+
+def other_part(weights, images, logs, out):
+    step = weights.shape[1]
+    out[:step] = slim(dot(weights, images[...], ((0,), (0,))))
     out[step:] = pieces(logs, images.shape[1])
 
 
-def rest_kernel(rows, weights, images, row_logs, base, out2, out3):
-    step = weights.shape[1] // 4
+def rest_kernel(rows, exps, images, first, row_total, column_total, row_logs, *outs):
+    weights, base, out2, out3 = outs
+    step = exps.shape[1] // 4
+    row_total, column_total = row_total[...], column_total[...]
     for b, out in ((3, out3), (2, out2)):
-        other_part(weights, images, b, row_logs[:, :1], out)
+        weigh(rows, exps, row_total, column_total, b, weights, b * step)
+        other_part(weights[:, b * step : (b + 1) * step], images, row_logs[:, :1], out)
+    weigh(rows, exps, row_total, column_total, 0, weights)
     base[...] = dot(weights[:, :step], images[...], ((0,), (0,)))
-
-
-def image_kernel(rows, weights, others, column_logs, sent, kept):
+    weights[:, step : 2 * step] = first[...]
+
+
+def image_kernel(rows, weights, others, column_total, sent, kept, logs):
     core = lax.axis_index("core")
     two = 2 * rows
-
-    def part(p, n=1):
-        return dot(weights[p * two : (p + n) * two], others[...], ((1,), (0,)))
-
-    own, upper, lower = part(0), part(1, 4), part(5, 3)
-    opposite = upper[3 * two :]
-    own_mine, own_other = ordered(core, own[:rows], own[rows:])
-    far_mine, far_other = ordered(core, opposite[:rows], opposite[rows:])
-    sent[:rows] = slim(own_other)
-    sent[rows : 7 * rows] = slim(upper[: 3 * two])
-    sent[7 * rows : 8 * rows] = slim(far_other)
-    sent[8 * rows :] = pieces(column_logs[:, :1], others.shape[1])
-    kept[:rows] = own_mine
+    part = dot(weights[: 5 * two], others[...], ((1,), (0,)))
+    mine, other = ordered(core, part[:rows], part[rows:two])
+    kept[:rows] = mine
+    sent[:rows] = slim(other)
+    sent[rows : 7 * rows] = slim(part[two : 4 * two])
+    mine, other = ordered(core, part[4 * two : 9 * rows], part[9 * rows :])
+    kept[rows:] = mine
+    sent[7 * rows : 8 * rows] = slim(other)
+    total = sum_log(column_total[...])
+    sent[8 * rows :] = pieces(total, others.shape[1])
+    logs[...] = jnp.broadcast_to(total, logs.shape)
+
+
+def lower_kernel(rows, weights, others, kept, out):
+    two = 2 * rows
+    part = dot(weights[5 * two :], others[...], ((1,), (0,)))
+    out[:rows] = kept[:rows]
     for k in range(3):
-        kept[rows + k * two : rows + (k + 1) * two] = lower[(2 - k) * two : (3 - k) * two]
-    kept[7 * rows :] = far_mine
+        out[rows + k * two : rows + (k + 1) * two] = part[(2 - k) * two : (3 - k) * two]
+    out[7 * rows :] = kept[rows:]
 
 
 def chip_kernel(rows, kept, got, column_logs, near, sent, logs):
@@ -396,22 +416,31 @@
     got = {k: along_second(columns, k) for k in (1, 3, 2)}
 
     packet, log = ((bundle + NOTE, width), bf16), ((1, 128), f32)
-    weights, row_logs, column_logs, first = local(
+    first, row_total, column_total, row_logs, packet1 = local(
         other_kernel,
         (exps, images, three, rows_below, rows_above, columns, got[1], got[2], got[3]),
+        ((count, across // 4), bf16),
+        ((1, count), f32),
+        column_shape,
+        log,
+        packet,
+    )
+    weights, base, *packets = local(
+        rest_kernel,
+        (exps, images, first, row_total, column_total, row_logs),
         ((count, across), bf16),
-        log,
-        log,
-        packet,
-    )
-    base, *packets = local(
-        rest_kernel, (weights, images, row_logs), ((bundle, width), f32), packet, packet
-    )
-    packets = [first, *packets]
+        ((bundle, width), f32),
+        packet,
+        packet,
+    )
+    packets = [packet1, *packets]
     seconds = {k: along_second(packets[k - 1], -k) for k in (1, 3, 2)}
 
-    sent, kept = local(image_kernel, (weights, others, column_logs), packet, ((bundle, width), f32))
+    sent, kept, column_logs = local(
+        image_kernel, (weights, others, column_total), packet, ((pair, width), f32), log
+    )
     got = swap(sent)
+    (kept,) = local(lower_kernel, (weights, others, kept), ((bundle, width), f32))
     around, sent, column_logs = local(
         chip_kernel,
         (kept, got, column_logs),

time: 103 us -> 99.1 us (0.962)
  the two profiles are of different devices: /device:TPU:1 before, /device:TPU:24 now
where the time goes in v3:
time: 99.1 us; the launch traced here: 97.4 us
  starting transfers between devices  47.9 us (48%)
  waiting for transfers between devices  37.8 us (38%)
  Pallas kernels  10.7 us (11%)
    ppermute x32, starting transfers between devices, send(): return lax.ppermute(array, AXES, pairs)  47.9 us
    ppermute x32, waiting for transfers between devices, send(): return lax.ppermute(array, AXES, pairs)  37.8 us
    pallas_call x16, Pallas kernels, run(): made(*(pltpu.with_memory_space_constraint(a, kept_in) for a in arrays))  10.7 us
  transfers between devices with their start and end apart: 32, of which 17 were waited for; matrix products, arithmetic and copies ran while one was open for 0% of the time, Pallas kernels for 2%

profile of v3, /device:TPU:24, one launch (start us, length us, event | category | flops | bytes accessed | tf_op | source)
XLA Modules:
  0.0 97.4 jit_solution(4683417018047215229)
XLA Ops:
  4.7 1.7 %collective-permute-start.7 = (bf16[64,1024]{1,0:T(8,128)(2,1)S(1)}, bf16[64,1024]{1,0:T(8,128)(2,1)S(1)}, u32[]{:S(2)}, u32[]{:S(2)}) collective-permute-start(bf16[64,1024]{1,0:T(8,128)(2,1)S(1)} %get-tuple-element.48), channel_id=1, source_target_pairs={{0,3},{8,11},{16,19},{24,27},{32,35},{40,43},{48,51},{56,59},{128,... | collective-permute-start | bytes 393224 | tf_op jit(solution)/shard_map/ppermute | solution.py:32
  6.5 1.8 %collective-permute-start.6 = (bf16[64,1024]{1,0:T(8,128)(2,1)S(1)}, bf16[64,1024]{1,0:T(8,128)(2,1)S(1)}, u32[]{:S(2)}, u32[]{:S(2)}) collective-permute-start(bf16[64,1024]{1,0:T(8,128)(2,1)S(1)} %get-tuple-element.48), channel_id=1, source_target_pairs={{0,2},{8,10},{16,18},{24,26},{32,34},{40,42},{48,50},{56,58},{128,... | collective-permute-start | bytes 393224 | tf_op jit(solution)/shard_map/ppermute | solution.py:32
  9.5 3.5 %collective-permute-done.6 = bf16[64,1024]{1,0:T(8,128)(2,1)S(1)} collective-permute-done((bf16[64,1024]{1,0:T(8,128)(2,1)S(1)}, bf16[64,1024]{1,0:T(8,128)(2,1)S(1)}, u32[]{:S(2)}, u32[]{:S(2)}) %collective-permute-start.6) | collective-permute-done | bytes 131104 | tf_op jit(solution)/shard_map/ppermute | solution.py:32
  13.0 2.0 %collective-permute-start.8 = (bf16[256,1024]{1,0:T(8,128)(2,1)S(1)}, bf16[256,1024]{1,0:T(8,128)(2,1)S(1)}, u32[]{:S(2)}, u32[]{:S(2)}) collective-permute-start(bf16[256,1024]{1,0:T(8,128)(2,1)S(1)} %get-tuple-element.86), channel_id=1, source_target_pairs={{0,128},{8,136},{16,144},{24,152},{32,160},{40,168},{48,176},{56,1... | collective-permute-start | bytes 1572872 | tf_op jit(solution)/shard_map/ppermute | solution.py:32
  16.6 1.9 %collective-permute-start.1 = (bf16[64,1024]{1,0:T(8,128)(2,1)S(1)}, bf16[64,1024]{1,0:T(8,128)(2,1)S(1)}, u32[]{:S(2)}, u32[]{:S(2)}) collective-permute-start(bf16[64,1024]{1,0:T(8,128)(2,1)S(1)} %get-tuple-element.47.refs_0_), channel_id=1, source_target_pairs={{0,8},{8,16},{16,24},{24,32},{32,40},{40,48},{48,56},{56,0},{128,1... | collective-permute-start | bytes 393224 | tf_op jit(solution)/shard_map/ppermute | solution.py:32
  18.5 2.6 %collective-permute-start.9 = (bf16[256,1024]{1,0:T(8,128)(2,1)S(1)}, bf16[256,1024]{1,0:T(8,128)(2,1)S(1)}, u32[]{:S(2)}, u32[]{:S(2)}) collective-permute-start(bf16[256,1024]{1,0:T(8,128)(2,1)S(1)} %get-tuple-element.86), channel_id=1, source_target_pairs={{0,4},{8,12},{16,20},{24,28},{32,36},{40,44},{48,52},{56,60},{128,... | collective-permute-start | bytes 1572872 | tf_op jit(solution)/shard_map/ppermute | solution.py:32
  22.7 2.3 %collective-permute-done.1.refs_0_ = bf16[64,1024]{1,0:T(8,128)(2,1)S(1)} collective-permute-done((bf16[64,1024]{1,0:T(8,128)(2,1)S(1)}, bf16[64,1024]{1,0:T(8,128)(2,1)S(1)}, u32[]{:S(2)}, u32[]{:S(2)}) %collective-permute-start.1) | collective-permute-done | bytes 131104 | tf_op jit(solution)/shard_map/ppermute | solution.py:32
  26.1 1.8 %collective-permute-start.10 = (bf16[256,1024]{1,0:T(8,128)(2,1)S(1)}, bf16[256,1024]{1,0:T(8,128)(2,1)S(1)}, u32[]{:S(2)}, u32[]{:S(2)}) collective-permute-start(bf16[256,1024]{1,0:T(8,128)(2,1)S(1)} %get-tuple-element.86), channel_id=1, source_target_pairs={{0,132},{8,140},{16,148},{24,156},{32,164},{40,172},{48,180},{56,1... | collective-permute-start | bytes 1572872 | tf_op jit(solution)/shard_map/ppermute | solution.py:32
  27.9 6.7 %collective-permute-done.3.refs_2_ = bf16[96,1024]{1,0:T(8,128)(2,1)S(1)} collective-permute-done((bf16[96,1024]{1,0:T(8,128)(2,1)S(1)}, bf16[96,1024]{1,0:T(8,128)(2,1)S(1)}, u32[]{:S(2)}, u32[]{:S(2)}) %collective-permute-start.3) | collective-permute-done | bytes 196640 | tf_op jit(solution)/shard_map/ppermute | solution.py:32
  34.9 1.6 %collective-permute-done.10 = bf16[256,1024]{1,0:T(8,128)(2,1)S(1)} collective-permute-done((bf16[256,1024]{1,0:T(8,128)(2,1)S(1)}, bf16[256,1024]{1,0:T(8,128)(2,1)S(1)}, u32[]{:S(2)}, u32[]{:S(2)}) %collective-permute-start.10) | collective-permute-done | bytes 524320 | tf_op jit(solution)/shard_map/ppermute | solution.py:32
  36.6 3.3 %shard_map.70 = (bf16[512,1024]{1,0:T(8,128)(2,1)S(1)}, f32[512,1024]{1,0:T(8,128)S(1)}, f32[1,640]{1,0:T(1,128)S(1)}, f32[1,1024]{1,0:T(1,128)S(1)}) custom-call(bf16[64,1024]{1,0:T(8,128)(2,1)S(1)} %get-tuple-element.47.refs_0_, bf16[224,1024]{1,0:T(8,128)(2,1)S(1)} %shard_map.69.refs_1_, bf16[224,1024]{1,0:T(8,128)(2,1)S(1)} %collective-permute-done.4.refs_2_, ...), custom_call_target="tpu_custom_call" | custom-call | tf_op jit(solution)/shard_map/pallas_call | solution.py:65
  47.2 1.9 %collective-permute-start.20 = (f32[1,1024]{1,0:T(1,128)S(1)}, f32[1,1024]{1,0:T(1,128)S(1)}, u32[]{:S(2)}, u32[]{:S(2)}) collective-permute-start(f32[1,1024]{1,0:T(1,128)S(1)} %shard_map.72.refs_5_), channel_id=1, source_target_pairs={{0,132},{8,140},{16,148},{24,156},{32,164},{40,172},{48,180},{56,1... | collective-permute-start | bytes 12296 | tf_op jit(solution)/shard_map/ppermute | solution.py:32
  50.3 2.2 %collective-permute-start.18 = (f32[1,1024]{1,0:T(1,128)S(1)}, f32[1,1024]{1,0:T(1,128)S(1)}, u32[]{:S(2)}, u32[]{:S(2)}) collective-permute-start(f32[1,1024]{1,0:T(1,128)S(1)} %shard_map.72.refs_5_), channel_id=1, source_target_pairs={{0,128},{8,136},{16,144},{24,152},{32,160},{40,168},{48,176},{56,1... | collective-permute-start | bytes 12296 | tf_op jit(solution)/shard_map/ppermute | solution.py:32
  52.6 1.9 %collective-permute-start.14 = (f32[1,640]{1,0:T(1,128)S(1)}, f32[1,640]{1,0:T(1,128)S(1)}, u32[]{:S(2)}, u32[]{:S(2)}) collective-permute-start(f32[1,640]{1,0:T(1,128)S(1)} %get-tuple-element.53), channel_id=1, source_target_pairs={{0,40},{8,48},{16,56},{24,0},{32,8},{40,16},{48,24},{56,32},{128,1... | collective-permute-start | bytes 7688 | tf_op jit(solution)/shard_map/ppermute | solution.py:32
  54.5 2.0 %collective-permute-start.13 = (f32[1,640]{1,0:T(1,128)S(1)}, f32[1,640]{1,0:T(1,128)S(1)}, u32[]{:S(2)}, u32[]{:S(2)}) collective-permute-start(f32[1,640]{1,0:T(1,128)S(1)} %get-tuple-element.52.refs_2_), channel_id=1, source_target_pairs={{0,24},{8,32},{16,40},{24,48},{32,56},{40,0},{48,8},{56,16},{128,1... | collective-permute-start | bytes 7688 | tf_op jit(solution)/shard_map/ppermute | solution.py:32
  58.1 3.1 %collective-permute-done.13.refs_3_ = f32[1,640]{1,0:T(1,128)S(1)} collective-permute-done((f32[1,640]{1,0:T(1,128)S(1)}, f32[1,640]{1,0:T(1,128)S(1)}, u32[]{:S(2)}, u32[]{:S(2)}) %collective-permute-start.13) | collective-permute-done | bytes 2592 | tf_op jit(solution)/shard_map/ppermute | solution.py:32
  62.1 1.8 %shard_map.74 = (bf16[512,1024]{1,0:T(8,128)(2,1)S(1)}, f32[256,1024]{1,0:T(8,128)S(1)}, bf16[264,1024]{1,0:T(8,128)(2,1)S(1)}, bf16[264,1024]{1,0:T(8,128)(2,1)S(1)}) custom-call(f32[512,1024]{1,0:T(8,128)S(1)} %get-tuple-element.49.refs_0_, bf16[512,1024]{1,0:T(8,128)(2,1)S(1)} %get-tuple-element.50.refs_1_, ...), custom_call_target="tpu_custom_call" | custom-call | tf_op jit(solution)/shard_map/pallas_call | solution.py:65
  64.8 2.2 %collective-permute-start.22 = (bf16[264,1024]{1,0:T(8,128)(2,1)S(1)}, bf16[264,1024]{1,0:T(8,128)(2,1)S(1)}, u32[]{:S(2)}, u32[]{:S(2)}) collective-permute-start(bf16[264,1024]{1,0:T(8,128)(2,1)S(1)} %get-tuple-element.61), channel_id=1, source_target_pairs={{0,4},{8,12},{16,20},{24,28},{32,36},{40,44},{48,52},{56,60},{128,... | collective-permute-start | bytes 1622024 | tf_op jit(solution)/shard_map/ppermute | solution.py:32
  69.8 3.9 %collective-permute-start.28 = (bf16[104,1024]{1,0:T(8,128)(2,1)S(1)}, bf16[104,1024]{1,0:T(8,128)(2,1)S(1)}, u32[]{:S(2)}, u32[]{:S(2)}) collective-permute-start(bf16[104,1024]{1,0:T(8,128)(2,1)S(1)} %get-tuple-element.72), channel_id=1, source_target_pairs={{0,48},{8,56},{16,0},{24,8},{32,16},{40,24},{48,32},{56,40},{128,1... | collective-permute-start | bytes 638984 | tf_op jit(solution)/shard_map/ppermute | solution.py:32
  73.8 2.1 %collective-permute-done.22.refs_2_ = bf16[264,1024]{1,0:T(8,128)(2,1)S(1)} collective-permute-done((bf16[264,1024]{1,0:T(8,128)(2,1)S(1)}, bf16[264,1024]{1,0:T(8,128)(2,1)S(1)}, u32[]{:S(2)}, u32[]{:S(2)}) %collective-permute-start.22) | collective-permute-done | bytes 540704 | tf_op jit(solution)/shard_map/ppermute | solution.py:32
  75.9 3.7 %collective-permute-done.23.refs_3_ = bf16[264,1024]{1,0:T(8,128)(2,1)S(1)} collective-permute-done((bf16[264,1024]{1,0:T(8,128)(2,1)S(1)}, bf16[264,1024]{1,0:T(8,128)(2,1)S(1)}, u32[]{:S(2)}, u32[]{:S(2)}) %collective-permute-start.23) | collective-permute-done | bytes 540704 | tf_op jit(solution)/shard_map/ppermute | solution.py:32
  79.6 2.0 %collective-permute-done.21.refs_1_ = bf16[264,1024]{1,0:T(8,128)(2,1)S(1)} collective-permute-done((bf16[264,1024]{1,0:T(8,128)(2,1)S(1)}, bf16[264,1024]{1,0:T(8,128)(2,1)S(1)}, u32[]{:S(2)}, u32[]{:S(2)}) %collective-permute-start.21) | collective-permute-done | bytes 540704 | tf_op jit(solution)/shard_map/ppermute | solution.py:32
  87.1 3.7 %collective-permute-start.30 = (bf16[72,1024]{1,0:T(8,128)(2,1)S(1)}, bf16[72,1024]{1,0:T(8,128)(2,1)S(1)}, u32[]{:S(2)}, u32[]{:S(2)}) collective-permute-start(bf16[72,1024]{1,0:T(8,128)(2,1)S(1)} %get-tuple-element.75), channel_id=1, source_target_pairs={{0,48},{8,56},{16,0},{24,8},{32,16},{40,24},{48,32},{56,40},{128,1... | collective-permute-start | bytes 442376 | tf_op jit(solution)/shard_map/ppermute | solution.py:32
  91.7 3.0 %collective-permute-done.30.refs_6_ = bf16[72,1024]{1,0:T(8,128)(2,1)S(1)} collective-permute-done((bf16[72,1024]{1,0:T(8,128)(2,1)S(1)}, bf16[72,1024]{1,0:T(8,128)(2,1)S(1)}, u32[]{:S(2)}, u32[]{:S(2)}) %collective-permute-start.30) | collective-permute-done | bytes 147488 | tf_op jit(solution)/shard_map/ppermute | solution.py:32
  (63 shorter events, 33.9 us)
Async XLA Ops:
  3.2 6.3 %collective-permute-start.5 = (bf16[64,1024]{1,0:T(8,128)(2,1)S(1)}, bf16[64,1024]{1,0:T(8,128)(2,1)S(1)}, u32[]{:S(2)}, u32[]{:S(2)}) collective-permute-start(bf16[64,1024]{1,0:T(8,128)(2,1)S(1)} %get-tuple-element.48), channel_id=1, source_target_pairs={{0,1},{8,9},{16,17},{24,25},{32,33},{40,41},{48,49},{56,57},{128,1... | collective-permute-start | bytes 393224 | tf_op jit(solution)/shard_map/ppermute | solution.py:32
  4.7 8.2 %collective-permute-start.7 = (bf16[64,1024]{1,0:T(8,128)(2,1)S(1)}, bf16[64,1024]{1,0:T(8,128)(2,1)S(1)}, u32[]{:S(2)}, u32[]{:S(2)}) collective-permute-start(bf16[64,1024]{1,0:T(8,128)(2,1)S(1)} %get-tuple-element.48), channel_id=1, source_target_pairs={{0,3},{8,11},{16,19},{24,27},{32,35},{40,43},{48,51},{56,59},{128,... | collective-permute-start | bytes 393224 | tf_op jit(solution)/shard_map/ppermute | solution.py:32
  6.5 6.5 %collective-permute-start.6 = (bf16[64,1024]{1,0:T(8,128)(2,1)S(1)}, bf16[64,1024]{1,0:T(8,128)(2,1)S(1)}, u32[]{:S(2)}, u32[]{:S(2)}) collective-permute-start(bf16[64,1024]{1,0:T(8,128)(2,1)S(1)} %get-tuple-element.48), channel_id=1, source_target_pairs={{0,2},{8,10},{16,18},{24,26},{32,34},{40,42},{48,50},{56,58},{128,... | collective-permute-start | bytes 393224 | tf_op jit(solution)/shard_map/ppermute | solution.py:32
  13.0 21.8 %collective-permute-start.8 = (bf16[256,1024]{1,0:T(8,128)(2,1)S(1)}, bf16[256,1024]{1,0:T(8,128)(2,1)S(1)}, u32[]{:S(2)}, u32[]{:S(2)}) collective-permute-start(bf16[256,1024]{1,0:T(8,128)(2,1)S(1)} %get-tuple-element.86), channel_id=1, source_target_pairs={{0,128},{8,136},{16,144},{24,152},{32,160},{40,168},{48,176},{56,1... | collective-permute-start | bytes 1572872 | tf_op jit(solution)/shard_map/ppermute | solution.py:32
  15.0 7.6 %collective-permute-start.2 = (bf16[64,1024]{1,0:T(8,128)(2,1)S(1)}, bf16[64,1024]{1,0:T(8,128)(2,1)S(1)}, u32[]{:S(2)}, u32[]{:S(2)}) collective-permute-start(bf16[64,1024]{1,0:T(8,128)(2,1)S(1)} %get-tuple-element.47.refs_0_), channel_id=1, source_target_pairs={{0,16},{8,24},{16,32},{24,40},{32,48},{40,56},{48,0},{56,8},{128,1... | collective-permute-start | bytes 393224 | tf_op jit(solution)/shard_map/ppermute | solution.py:32
  16.6 8.3 %collective-permute-start.1 = (bf16[64,1024]{1,0:T(8,128)(2,1)S(1)}, bf16[64,1024]{1,0:T(8,128)(2,1)S(1)}, u32[]{:S(2)}, u32[]{:S(2)}) collective-permute-start(bf16[64,1024]{1,0:T(8,128)(2,1)S(1)} %get-tuple-element.47.refs_0_), channel_id=1, source_target_pairs={{0,8},{8,16},{16,24},{24,32},{32,40},{40,48},{48,56},{56,0},{128,1... | collective-permute-start | bytes 393224 | tf_op jit(solution)/shard_map/ppermute | solution.py:32
  18.5 16.3 %collective-permute-start.9 = (bf16[256,1024]{1,0:T(8,128)(2,1)S(1)}, bf16[256,1024]{1,0:T(8,128)(2,1)S(1)}, u32[]{:S(2)}, u32[]{:S(2)}) collective-permute-start(bf16[256,1024]{1,0:T(8,128)(2,1)S(1)} %get-tuple-element.86), channel_id=1, source_target_pairs={{0,4},{8,12},{16,20},{24,28},{32,36},{40,44},{48,52},{56,60},{128,... | collective-permute-start | bytes 1572872 | tf_op jit(solution)/shard_map/ppermute | solution.py:32
  25.0 9.7 %collective-permute-start.3 = (bf16[96,1024]{1,0:T(8,128)(2,1)S(1)}, bf16[96,1024]{1,0:T(8,128)(2,1)S(1)}, u32[]{:S(2)}, u32[]{:S(2)}) collective-permute-start(bf16[96,1024]{1,0:T(8,128)(2,1)S(1)} %shard_map.68), channel_id=1, source_target_pairs={{0,16},{8,24},{16,32},{24,40},{32,48},{40,56},{48,0},{56,8},{128,1... | collective-permute-start | bytes 589832 | tf_op jit(solution)/shard_map/ppermute | solution.py:32
  26.1 10.4 %collective-permute-start.10 = (bf16[256,1024]{1,0:T(8,128)(2,1)S(1)}, bf16[256,1024]{1,0:T(8,128)(2,1)S(1)}, u32[]{:S(2)}, u32[]{:S(2)}) collective-permute-start(bf16[256,1024]{1,0:T(8,128)(2,1)S(1)} %get-tuple-element.86), channel_id=1, source_target_pairs={{0,132},{8,140},{16,148},{24,156},{32,164},{40,172},{48,180},{56,1... | collective-permute-start | bytes 1572872 | tf_op jit(solution)/shard_map/ppermute | solution.py:32
  43.2 9.3 %collective-permute-start.12 = (f32[1,640]{1,0:T(1,128)S(1)}, f32[1,640]{1,0:T(1,128)S(1)}, u32[]{:S(2)}, u32[]{:S(2)}) collective-permute-start(f32[1,640]{1,0:T(1,128)S(1)} %get-tuple-element.51.refs_0_), channel_id=1, source_target_pairs={{0,56},{8,0},{16,8},{24,16},{32,24},{40,32},{48,40},{56,48},{128,1... | collective-permute-start | bytes 7688 | tf_op jit(solution)/shard_map/ppermute | solution.py:32
  44.8 7.7 %collective-permute-start.11 = (f32[1,640]{1,0:T(1,128)S(1)}, f32[1,640]{1,0:T(1,128)S(1)}, u32[]{:S(2)}, u32[]{:S(2)}) collective-permute-start(f32[1,640]{1,0:T(1,128)S(1)} %get-tuple-element.51.refs_0_), channel_id=1, source_target_pairs={{0,8},{8,16},{16,24},{24,32},{32,40},{40,48},{48,56},{56,0},{128,1... | collective-permute-start | bytes 7688 | tf_op jit(solution)/shard_map/ppermute | solution.py:32
  47.2 13.9 %collective-permute-start.20 = (f32[1,1024]{1,0:T(1,128)S(1)}, f32[1,1024]{1,0:T(1,128)S(1)}, u32[]{:S(2)}, u32[]{:S(2)}) collective-permute-start(f32[1,1024]{1,0:T(1,128)S(1)} %shard_map.72.refs_5_), channel_id=1, source_target_pairs={{0,132},{8,140},{16,148},{24,156},{32,164},{40,172},{48,180},{56,1... | collective-permute-start | bytes 12296 | tf_op jit(solution)/shard_map/ppermute | solution.py:32
  49.1 12.0 %collective-permute-start.19 = (f32[1,1024]{1,0:T(1,128)S(1)}, f32[1,1024]{1,0:T(1,128)S(1)}, u32[]{:S(2)}, u32[]{:S(2)}) collective-permute-start(f32[1,1024]{1,0:T(1,128)S(1)} %shard_map.72.refs_5_), channel_id=1, source_target_pairs={{0,4},{8,12},{16,20},{24,28},{32,36},{40,44},{48,52},{56,60},{128,... | collective-permute-start | bytes 12296 | tf_op jit(solution)/shard_map/ppermute | solution.py:32
  50.3 10.8 %collective-permute-start.18 = (f32[1,1024]{1,0:T(1,128)S(1)}, f32[1,1024]{1,0:T(1,128)S(1)}, u32[]{:S(2)}, u32[]{:S(2)}) collective-permute-start(f32[1,1024]{1,0:T(1,128)S(1)} %shard_map.72.refs_5_), channel_id=1, source_target_pairs={{0,128},{8,136},{16,144},{24,152},{32,160},{40,168},{48,176},{56,1... | collective-permute-start | bytes 12296 | tf_op jit(solution)/shard_map/ppermute | solution.py:32
  54.5 6.6 %collective-permute-start.13 = (f32[1,640]{1,0:T(1,128)S(1)}, f32[1,640]{1,0:T(1,128)S(1)}, u32[]{:S(2)}, u32[]{:S(2)}) collective-permute-start(f32[1,640]{1,0:T(1,128)S(1)} %get-tuple-element.52.refs_2_), channel_id=1, source_target_pairs={{0,24},{8,32},{16,40},{24,48},{32,56},{40,0},{48,8},{56,16},{128,1... | collective-permute-start | bytes 7688 | tf_op jit(solution)/shard_map/ppermute | solution.py:32
  64.8 11.0 %collective-permute-start.22 = (bf16[264,1024]{1,0:T(8,128)(2,1)S(1)}, bf16[264,1024]{1,0:T(8,128)(2,1)S(1)}, u32[]{:S(2)}, u32[]{:S(2)}) collective-permute-start(bf16[264,1024]{1,0:T(8,128)(2,1)S(1)} %get-tuple-element.61), channel_id=1, source_target_pairs={{0,4},{8,12},{16,20},{24,28},{32,36},{40,44},{48,52},{56,60},{128,... | collective-permute-start | bytes 1622024 | tf_op jit(solution)/shard_map/ppermute | solution.py:32
  67.0 12.6 %collective-permute-start.23 = (bf16[264,1024]{1,0:T(8,128)(2,1)S(1)}, bf16[264,1024]{1,0:T(8,128)(2,1)S(1)}, u32[]{:S(2)}, u32[]{:S(2)}) collective-permute-start(bf16[264,1024]{1,0:T(8,128)(2,1)S(1)} %get-tuple-element.62), channel_id=1, source_target_pairs={{0,128},{8,136},{16,144},{24,152},{32,160},{40,168},{48,176},{56,1... | collective-permute-start | bytes 1622024 | tf_op jit(solution)/shard_map/ppermute | solution.py:32
  67.6 14.0 %collective-permute-start.21 = (bf16[264,1024]{1,0:T(8,128)(2,1)S(1)}, bf16[264,1024]{1,0:T(8,128)(2,1)S(1)}, u32[]{:S(2)}, u32[]{:S(2)}) collective-permute-start(bf16[264,1024]{1,0:T(8,128)(2,1)S(1)} %get-tuple-element.60), channel_id=1, source_target_pairs={{0,132},{8,140},{16,148},{24,156},{32,164},{40,172},{48,180},{56,1... | collective-permute-start | bytes 1622024 | tf_op jit(solution)/shard_map/ppermute | solution.py:32
  69.8 15.7 %collective-permute-start.28 = (bf16[104,1024]{1,0:T(8,128)(2,1)S(1)}, bf16[104,1024]{1,0:T(8,128)(2,1)S(1)}, u32[]{:S(2)}, u32[]{:S(2)}) collective-permute-start(bf16[104,1024]{1,0:T(8,128)(2,1)S(1)} %get-tuple-element.72), channel_id=1, source_target_pairs={{0,48},{8,56},{16,0},{24,8},{32,16},{40,24},{48,32},{56,40},{128,1... | collective-permute-start | bytes 638984 | tf_op jit(solution)/shard_map/ppermute | solution.py:32
  82.0 8.8 %collective-permute-start.24 = (bf16[72,1024]{1,0:T(8,128)(2,1)S(1)}, bf16[72,1024]{1,0:T(8,128)(2,1)S(1)}, u32[]{:S(2)}, u32[]{:S(2)}) collective-permute-start(bf16[72,1024]{1,0:T(8,128)(2,1)S(1)} %get-tuple-element.64), channel_id=1, source_target_pairs={{0,3},{8,11},{16,19},{24,27},{32,35},{40,43},{48,51},{56,59},{128,... | collective-permute-start | bytes 442376 | tf_op jit(solution)/shard_map/ppermute | solution.py:32
  83.5 7.3 %collective-permute-start.25 = (bf16[72,1024]{1,0:T(8,128)(2,1)S(1)}, bf16[72,1024]{1,0:T(8,128)(2,1)S(1)}, u32[]{:S(2)}, u32[]{:S(2)}) collective-permute-start(bf16[72,1024]{1,0:T(8,128)(2,1)S(1)} %get-tuple-element.65), channel_id=1, source_target_pairs={{0,2},{8,10},{16,18},{24,26},{32,34},{40,42},{48,50},{56,58},{128,... | collective-permute-start | bytes 442376 | tf_op jit(solution)/shard_map/ppermute | solution.py:32
  85.0 6.7 %collective-permute-start.26 = (bf16[72,1024]{1,0:T(8,128)(2,1)S(1)}, bf16[72,1024]{1,0:T(8,128)(2,1)S(1)}, u32[]{:S(2)}, u32[]{:S(2)}) collective-permute-start(bf16[72,1024]{1,0:T(8,128)(2,1)S(1)} %get-tuple-element.66), channel_id=1, source_target_pairs={{0,1},{8,9},{16,17},{24,25},{32,33},{40,41},{48,49},{56,57},{128,1... | collective-permute-start | bytes 442376 | tf_op jit(solution)/shard_map/ppermute | solution.py:32
  85.7 6.1 %collective-permute-start.29 = (bf16[72,1024]{1,0:T(8,128)(2,1)S(1)}, bf16[72,1024]{1,0:T(8,128)(2,1)S(1)}, u32[]{:S(2)}, u32[]{:S(2)}) collective-permute-start(bf16[72,1024]{1,0:T(8,128)(2,1)S(1)} %get-tuple-element.74), channel_id=1, source_target_pairs={{0,56},{8,0},{16,8},{24,16},{32,24},{40,32},{48,40},{56,48},{128,1... | collective-permute-start | bytes 442376 | tf_op jit(solution)/shard_map/ppermute | solution.py:32
  87.1 7.7 %collective-permute-start.30 = (bf16[72,1024]{1,0:T(8,128)(2,1)S(1)}, bf16[72,1024]{1,0:T(8,128)(2,1)S(1)}, u32[]{:S(2)}, u32[]{:S(2)}) collective-permute-start(bf16[72,1024]{1,0:T(8,128)(2,1)S(1)} %get-tuple-element.75), channel_id=1, source_target_pairs={{0,48},{8,56},{16,0},{24,8},{32,16},{40,24},{48,32},{56,40},{128,1... | collective-permute-start | bytes 442376 | tf_op jit(solution)/shard_map/ppermute | solution.py:32
  (8 other events, 30.5 us)
